TPU v7x, 32 devices: a whole 2x2x4 slice. The times are simulated.
32 devices in a mesh: sub: 16 (over z, x, core), chan: 2 (over y).
Axes of the slice: x: 2, y: 2, z: 4, core: 2. Of those that a mesh axis runs over, the one named last changes fastest.
Arguments:
- raw_pulses: bfloat16 [2, 512, 2, 2048], P(None, 'sub', 'chan'), may hold values from -6 to 6
- range_filter: bfloat16 [2, 2048, 1024], P(None, ('sub', 'chan')), may hold values from -0.09375 to 0.09375
- channel_mix: float32 [2, 32, 2, 2], replicated, may hold values from -3 to 3
- steer_angles: float32 [256], replicated, may hold values from -3.140625 to 3.140625
- band_offsets: int32 [4, 512], replicated, may hold values from 0 to 248
- band_weights: float32 [4, 2, 2, 512, 8], replicated, may hold values from -1 to 1
- smoothing: float32 [4096], P('sub'), may hold values from 0.3 to 0.5
Outputs:
- despeckled: float32 [4096, 1024], P('sub', 'chan')
All inputs are finite; a program needn't handle non-finite values.
Results may differ from a plain program's by a relative error of at most 0.0036.
Values may be sent and summed in bfloat16 or wider, within the bound.
A program may use at most 64 MiB of HBM per device.

v0:
```python
import jax
import jax.numpy as jnp
import numpy as np
from jax import lax
from jax.experimental import pallas as pl
from jax.sharding import PartitionSpec as P

PASSES = 3
HIGH = lax.Precision.HIGHEST
LOW = jnp.bfloat16


def rounded(value):
    return lax.reduce_precision(value, exponent_bits=8, mantissa_bits=7)


def halves(value):
    top = rounded(value)
    return top.astype(LOW), (value - top).astype(LOW)


def doppler_table(count):
    index_row = jnp.arange(count, dtype=jnp.int32)
    product = index_row[:, None] * index_row[None, :] % count
    phase = 2.0 * np.pi / count * product.astype(jnp.float32)
    factor = 1.0 / np.sqrt(count)
    return (
        rounded(jnp.cos(phase) * factor),
        rounded(-jnp.sin(phase) * factor),
    )


def steer_table(steer_angles, count):
    offsets = jnp.arange(count, dtype=jnp.int32).astype(jnp.float32) - 0.5 * count
    phase = offsets[:, None] * steer_angles[None, :]
    factor = 1.0 / np.sqrt(count)
    return (
        rounded(jnp.cos(phase) * factor),
        rounded(jnp.sin(phase) * factor),
    )


def forming_operator(channel_mix, steer_angles, pulse_count):
    channels = channel_mix.shape[2]
    dop_r, dop_i = doppler_table(pulse_count)
    beam_r, beam_i = steer_table(steer_angles, channels * pulse_count)
    mix = channel_mix.transpose(0, 3, 2, 1)[:, :, None, :, :]
    dr, di = dop_r.T[None, :, None, :], dop_i.T[None, :, None, :]
    shape = (channels * pulse_count, channels * pulse_count)
    mixed_r = (mix[0] * dr - mix[1] * di).reshape(shape)
    mixed_i = (mix[0] * di + mix[1] * dr).reshape(shape)
    left = jnp.concatenate([mixed_r, mixed_i], axis=1)
    t_r = jnp.dot(left, jnp.concatenate([beam_r, -beam_i], axis=0), precision=HIGH)
    t_i = jnp.dot(left, jnp.concatenate([beam_i, beam_r], axis=0), precision=HIGH)
    angles = steer_angles.shape[0]
    t_r = t_r.reshape(channels, pulse_count, angles)
    t_i = t_i.reshape(channels, pulse_count, angles)
    top = jnp.concatenate([t_r, t_i], axis=2)
    low = jnp.concatenate([-t_i, t_r], axis=2)
    both = jnp.concatenate([top, low], axis=1)
    return both.reshape(channels * 2 * pulse_count, 2 * angles)


def operator_body(offsets_ref, weights_ref, *out_refs):
    band_width, count = weights_ref.shape[3], weights_ref.shape[4]
    delta = lax.broadcasted_iota(jnp.int32, (count, count), 0) - offsets_ref[0]
    bands = [jnp.zeros((count, count), jnp.float32)] * 2
    for j in range(band_width):
        hit = delta == j
        bands = [
            jnp.where(hit, weights_ref[0, 0, part, j : j + 1, :], bands[part]) for part in range(2)
        ]
    for order, ref in enumerate(out_refs):
        real, imag = (band.astype(LOW) for band in bands)
        ref[0, 0, :count, :count] = real
        ref[0, 0, :count, count:] = imag
        ref[0, 0, count:, :count] = -imag
        ref[0, 0, count:, count:] = real
        if order + 1 < len(out_refs):
            bands = [band - band.astype(LOW).astype(jnp.float32) for band in bands]


def merge_operators(offsets, weights, parts):
    levels, _, _, merged, band_width = weights.shape
    count = merged // 2
    by_step = weights.transpose(0, 1, 2, 4, 3)
    shape = jax.ShapeDtypeStruct((levels, 2, 2 * count, 2 * merged), LOW)
    return pl.pallas_call(
        operator_body,
        grid=(levels, 2, 2),
        in_specs=[
            pl.BlockSpec((1, 1, count), lambda l, c, h: (l, 0, h)),
            pl.BlockSpec((1, 1, 2, band_width, count), lambda l, c, h: (l, c, 0, 0, h)),
        ],
        out_specs=[
            pl.BlockSpec((1, 1, 2 * count, 2 * count), lambda l, c, h: (l, c, 0, h))
        ] * parts,
        out_shape=[shape] * parts,
        cost_estimate=pl.CostEstimate(
            flops=levels * 4 * count * count * 32,
            bytes_accessed=levels * parts * 16 * count * count * 2,
            transcendentals=0,
        ),
    )(offsets[:, None, :], by_step)


def low_dot(left, right):
    return jnp.dot(left, right, preferred_element_type=jnp.float32)


def local(
    raw_pulses, range_filter, channel_mix, steer_angles, band_offsets, band_weights, smoothing
):
    pulses = raw_pulses.shape[1]
    samples = raw_pulses.shape[3]
    bins = range_filter.shape[2]
    angles = steer_angles.shape[0]
    levels = band_offsets.shape[0]
    subs, chans = lax.axis_size("sub"), lax.axis_size("chan")
    own = bins // (subs * chans)

    part = lax.all_to_all(range_filter, "chan", split_axis=2, concat_axis=1, tiled=True)
    filt = lax.all_gather(part, "sub", axis=1, tiled=True)
    echo = lax.all_gather(raw_pulses[:, :, 0, :], "chan", axis=0)

    forming = forming_operator(channel_mix, steer_angles, pulses)
    form_top, form_low = halves(forming)
    base_top, base_low = merge_operators(band_offsets[:1], band_weights[:1], 2)
    folded = [
        low_dot(form_top, base_top[0, c])
        + (low_dot(form_low, base_top[0, c]) + low_dot(form_top, base_low[0, c]))
        for c in range(2)
    ]
    folded_top, folded_low = halves(jnp.concatenate(folded, axis=0))
    (later,) = merge_operators(band_offsets[1:], band_weights[1:], 1)

    real_rows = jnp.concatenate([echo[:, 0], -echo[:, 1]], axis=2)
    imag_rows = jnp.concatenate([echo[:, 1], echo[:, 0]], axis=2)
    stacked = jnp.concatenate([real_rows, imag_rows], axis=1).reshape(-1, 2 * samples)
    compressed = low_dot(stacked, filt.reshape(2 * samples, -1)).astype(LOW)
    blocks = compressed.T.reshape(subs, own, -1)
    got = lax.all_to_all(blocks, "sub", split_axis=0, concat_axis=0, tiled=True)
    image = got.reshape(subs * own, -1)
    for level in range(levels):
        run = (1 << level) * own
        wide = image.shape[1]
        field = image.astype(LOW).reshape(-1, 2, run, wide)
        pair = jnp.concatenate([field[:, 0], field[:, 1]], axis=2).reshape(-1, 2 * wide)
        if level == 0:
            out = low_dot(pair, folded_top) + low_dot(pair, folded_low)
        else:
            out = low_dot(pair, later[level - 1].reshape(2 * wide, -1))
        out = out.reshape(-1, run, 4 * angles)
        image = jnp.stack([out[:, :, : 2 * angles], out[:, :, 2 * angles :]], axis=1)
        image = image.reshape(-1, 2 * angles)
    power = image[:, :angles] * image[:, :angles] + image[:, angles:] * image[:, angles:]
    power = power.astype(LOW).reshape(subs, own, angles)
    power = lax.all_to_all(power, "sub", split_axis=0, concat_axis=0, tiled=True)
    power = power.reshape(subs * own, angles)
    up = [(i, i + 1) for i in range(chans - 1)]
    down = [(j, i) for i, j in up]
    before = lax.ppermute(power[-PASSES:], "chan", up).astype(jnp.float32)
    after = lax.ppermute(power[:PASSES], "chan", down).astype(jnp.float32)
    power = jnp.concatenate([before, power.astype(jnp.float32), after], axis=0)
    rate = smoothing[None, :]
    at = lax.axis_index("chan")
    lead, trail = at == 0, at == chans - 1
    for sweep in range(PASSES):
        mid = power[1:-1]
        power = mid + rate * (power[:-2] - 2.0 * mid + power[2:])
        edge = PASSES - 1 - sweep
        if edge:
            inner = power[edge:-edge]
            head = jnp.where(lead, 0.0, power[:edge])
            tail = jnp.where(trail, 0.0, power[-edge:])
            power = jnp.concatenate([head, inner, tail], axis=0)
    return power.T


def solution(mesh):
    in_specs = (
        P(None, "sub", "chan", None),
        P(None, ("sub", "chan"), None),
        P(),
        P(),
        P(),
        P(),
        P("sub"),
    )
    out_specs = P("sub", "chan")
    return jax.shard_map(local, mesh=mesh, in_specs=in_specs, out_specs=out_specs, check_vma=False)
```

profile of v0, /device:TPU:0, one launch (start us, length us, event | category | flops | bytes accessed | tf_op | source)
XLA Modules:
  0.0 119.9 jit_solution(8060832167545414871)
XLA Ops:
  6.5 1.3 %copy.42 = bf16[2,64,1024]{1,0,2:T(2,128)(2,1)S(1)} copy(bf16[2,64,1024]{2,1,0:T(8,128)(2,1)} %param.8) | data formatting | bytes 524288 | tf_op args[1]
  8.3 9.2 %all_to_all.28 = bf16[2,2,32768]{2,1,0:T(2,128)(2,1)S(1)} all-to-all(bf16[2,2,32768]{2,1,0:T(2,128)(2,1)S(1)} %reshape.197), channel_id=1, replica_groups=mesh['sub'=16,'chan'=2] {'chan'}, dimensions={0} | all-to-all | bytes 524288 | tf_op jit(solution)/shard_map/all_to_all | solution.py:122
  17.9 1.0 copy.44
  21.7 4.2 %shard_map.73 = (bf16[1,2,512,1024]{3,2,1,0:T(8,128)(2,1)}, bf16[1,2,512,1024]{3,2,1,0:T(8,128)(2,1)}) custom-call(s32[1,1,512]{2,1,0:T(1,128)} %slice_bitcast_fusion.18.offsets_ref, f32[1,2,2,8,512]{4,3,2,1,0:T(8,128)} %slice_bitcast_fusion.17.weights_ref), custom_call_target="tpu_custom_call" | custom-call | flops 8388608 | bytes 4194304 | tf_op jit(solution)/shard_map/pallas_call | solution.py:88
  26.6 9.0 %shard_map.74 = bf16[3,2,512,1024]{3,2,1,0:T(8,128)(2,1)} custom-call(s32[3,1,512]{2,1,0:T(1,128)} %broadcast_in_dim.26.offsets_ref, f32[3,2,2,8,512]{4,3,2,1,0:T(8,128)} %slice_bitcast_fusion.16.weights_ref), custom_call_target="tpu_custom_call" | custom-call | flops 25165824 | bytes 6291456 | tf_op jit(solution)/shard_map/pallas_call | solution.py:88
  35.9 7.4 %all-gather = bf16[4,32,1,2048]{3,1,2,0:T(8,128)(2,1)S(1)} all-gather(bf16[2,32,1,2048]{3,1,2,0:T(8,128)(2,1)S(1)} %copy-done.5), channel_id=2, replica_groups=mesh['sub'=16,'chan'=2] {'chan'}, dimensions={0}, use_global_device_ids=true | all-gather | bytes 786432 | tf_op jit(solution)/shard_map/all_gather | solution.py:124
  44.6 1.1 convolution_add_fusion.3
  45.7 1.7 %copy-done = bf16[3,2,512,1024]{3,2,1,0:T(8,128)(2,1)S(1)} copy-done((bf16[3,2,512,1024]{3,2,1,0:T(8,128)(2,1)S(1)}, bf16[3,2,512,1024]{3,2,1,0:T(8,128)(2,1)}, u32[]{:S(2)}) %copy-start) | copy-done | bytes 6291480
  47.5 3.0 %fusion.69 = (bf16[1,2,512,1024]{3,2,1,0:T(8,128)(2,1)}, bf16[1,2,512,1024]{3,2,1,0:T(8,128)(2,1)S(1)}, bf16[1,2,512,1024]{3,2,1,0:T(8,128)(2,1)}) fusion(bf16[3,2,512,1024]{3,2,1,0:T(8,128)(2,1)S(1)} %copy-done), kind=kLoop, calls=%fused_computation.136 | loop fusion | bytes 12582912 | tf_op jit(solution)/shard_map/slice | solution.py:152
  50.6 1.1 maximum_maximum_fusion
  51.7 18.1 %all-gather.3.cloned.1.call-done = bf16[2,2048,512]{2,1,0:T(8,128)(2,1)} async-done(((bf16[2,128,512]{2,1,0:T(8,128)(2,1)}), bf16[2,2048,512]{2,1,0:T(8,128)(2,1)}) %all-gather.3.cloned.1.call-update) | async-done | bytes 4194320 | tf_op jit(solution)/shard_map/all_gather | solution.py:123
  69.8 3.2 %fusion.1 = bf16[512,128]{0,1:T(8,128)(2,1)S(1)} fusion(bf16[128,4096]{1,0:T(8,128)(2,1)} %bitcast.132, bf16[4096,512]{1,0:T(8,128)(2,1)} %bitcast.131), kind=kOutput, calls=%fused_computation.12 | convolution fusion | flops 536936448 | bytes 5373952 | tf_op jit(solution)/shard_map/dot_general | solution.py:108
  73.1 0.7 copy.45
  73.8 3.5 %all-to-all-start.1 = ((bf16[16,32,128]{2,1,0:T(8,128)(2,1)}), bf16[16,32,128]{2,1,0:T(8,128)(2,1)S(1)}, u32[]{:S(2)}, u32[]{:S(2)}) async-start(bf16[16,32,128]{2,1,0:T(8,128)(2,1)} %bitcast.10), calls=%async_computation.1 | async-start | bytes 262144 | tf_op jit(solution)/shard_map/all_to_all | solution.py:142
  77.3 1.7 %convolution_add_fusion.4 = f32[128,1024]{1,0:T(8,128)S(1)} fusion(f32[128,1024]{1,0:T(8,128)} %convolution_add_fusion.3, bf16[128,512]{1,0:T(8,128)(2,1)S(1)} %bitcast.136, bf16[1,2,512,1024]{3,2,1,0:T(8,128)(2,1)} %get-tuple-element.7), kind=kOutput, calls=%fused_computation.10 | convolution fusion | flops 134348800 | bytes 2228224 | tf_op jit(solution)/shard_map/dot_general | solution.py:108
  79.0 6.2 %all-to-all-done.1 = bf16[16,32,128]{2,1,0:T(8,128)(2,1)S(1)} async-done(((bf16[16,32,128]{2,1,0:T(8,128)(2,1)}), bf16[16,32,128]{2,1,0:T(8,128)(2,1)S(1)}, u32[]{:S(2)}, u32[]{:S(2)}) %all-to-all-start.1) | async-done | bytes 131104 | tf_op jit(solution)/shard_map/all_to_all | solution.py:142
  86.0 1.4 %copy-done.4 = bf16[1,2,512,1024]{3,2,1,0:T(8,128)(2,1)S(1)} copy-done((bf16[1,2,512,1024]{3,2,1,0:T(8,128)(2,1)S(1)}, bf16[1,2,512,1024]{3,2,1,0:T(8,128)(2,1)}, u32[]{:S(2)}) %copy-start.4) | copy-done | bytes 2097176
  87.4 0.7 convolution_convert_fusion.1
  88.3 1.4 %copy-done.3 = bf16[1,2,512,1024]{3,2,1,0:T(8,128)(2,1)S(1)} copy-done((bf16[1,2,512,1024]{3,2,1,0:T(8,128)(2,1)S(1)}, bf16[1,2,512,1024]{3,2,1,0:T(8,128)(2,1)}, u32[]{:S(2)}) %copy-start.3) | copy-done | bytes 2097176
  91.6 12.6 %all_to_all.29 = bf16[16,32,256]{2,1,0:T(8,128)(2,1)S(1)} all-to-all(bf16[16,32,256]{2,1,0:T(8,128)(2,1)S(1)} %bitcast.152), channel_id=1, replica_groups=mesh['sub'=16,'chan'=2] {'sub'}, dimensions={0} | all-to-all | bytes 524288 | tf_op jit(solution)/shard_map/all_to_all | solution.py:158
  104.2 1.3 %collective-permute-start.1 = (bf16[3,256]{1,0:T(4,128)(2,1)S(1)}, bf16[3,256]{1,0:T(4,128)(2,1)S(1)}, u32[]{:S(2)}, u32[]{:S(2)}) collective-permute-start(bf16[3,256]{1,0:T(4,128)(2,1)S(1)} %get-tuple-element.33), channel_id=1, source_target_pairs={{1,0},{3,2},{5,4},{7,6},{9,8},{11,10},{13,12},{15,14},{17,16},{19,... | collective-permute-start | bytes 4616 | tf_op jit(solution)/shard_map/ppermute | solution.py:163
  105.5 4.5 %collective-permute-start = (bf16[3,256]{1,0:T(4,128)(2,1)S(1)}, bf16[3,256]{1,0:T(4,128)(2,1)S(1)}, u32[]{:S(2)}, u32[]{:S(2)}) collective-permute-start(bf16[3,256]{1,0:T(4,128)(2,1)S(1)} %get-tuple-element.32), channel_id=1, source_target_pairs={{0,1},{2,3},{4,5},{6,7},{8,9},{10,11},{12,13},{14,15},{16,17},{18,... | collective-permute-start | bytes 4616 | tf_op jit(solution)/shard_map/ppermute | solution.py:162
  110.1 1.3 %collective-permute-done = bf16[3,256]{1,0:T(4,128)(2,1)S(1)} collective-permute-done((bf16[3,256]{1,0:T(4,128)(2,1)S(1)}, bf16[3,256]{1,0:T(4,128)(2,1)S(1)}, u32[]{:S(2)}, u32[]{:S(2)}) %collective-permute-start) | collective-permute-done | bytes 1568 | tf_op jit(solution)/shard_map/ppermute | solution.py:162
  112.1 1.0 copy.57
  (75 shorter events, 9.2 us)
Async XLA Ops:
  6.5 12.4 %copy-start.7 = (s32[4,512]{1,0:T(4,128)S(1)}, s32[4,512]{1,0:T(4,128)}, u32[]{:S(2)}) copy-start(s32[4,512]{1,0:T(4,128)} %param.11) | copy-start | bytes 24580
  6.5 13.1 %copy-start.9 = (f32[2,32,2,2]{1,3,2,0:T(2,128)S(1)}, f32[2,32,2,2]{1,3,2,0:T(2,128)}, u32[]{:S(2)}) copy-start(f32[2,32,2,2]{1,3,2,0:T(2,128)} %param.9) | copy-start | bytes 3076
  6.5 13.4 %copy-start.10 = (f32[256]{0:T(256)S(1)}, f32[256]{0:T(256)}, u32[]{:S(2)}) copy-start(f32[256]{0:T(256)} %param.10) | copy-start | bytes 3076
  6.5 63.3 %all-gather.3.cloned.1.call-start = ((), (), s32[]{:S(2)}) async-start(), calls=%async_computation.3 | async-start | bytes 4456448 | tf_op jit(solution)/shard_map/all_gather | solution.py:123
  7.8 13.3 %copy-start.6 = (f32[4,2,2,512,8]{3,4,2,1,0:T(8,128)S(1)}, f32[4,2,2,512,8]{3,4,2,1,0:T(8,128)}, u32[]{:S(2)}) copy-start(f32[4,2,2,512,8]{3,4,2,1,0:T(8,128)} %param.12) | copy-start | bytes 786436
  26.6 9.3 %copy-start.5 = (bf16[2,32,1,2048]{3,1,2,0:T(8,128)(2,1)S(1)}, bf16[2,32,1,2048]{3,1,2,0:T(8,128)(2,1)}, u32[]{:S(2)}) copy-start(bf16[2,32,1,2048]{3,1,2,0:T(8,128)(2,1)} %param.7) | copy-start | bytes 786436
  26.6 16.7 %copy-start.1 = (bf16[1,2,512,1024]{3,2,1,0:T(8,128)(2,1)S(1)}, bf16[1,2,512,1024]{3,2,1,0:T(8,128)(2,1)}, u32[]{:S(2)}) copy-start(bf16[1,2,512,1024]{3,2,1,0:T(8,128)(2,1)} %get-tuple-element.7) | copy-start | bytes 6291460
  35.9 8.0 %copy-start.2 = (bf16[1,2,512,1024]{3,2,1,0:T(8,128)(2,1)S(1)}, bf16[1,2,512,1024]{3,2,1,0:T(8,128)(2,1)}, u32[]{:S(2)}) copy-start(bf16[1,2,512,1024]{3,2,1,0:T(8,128)(2,1)} %get-tuple-element.8) | copy-start | bytes 6291460
  44.0 3.5 %copy-start = (bf16[3,2,512,1024]{3,2,1,0:T(8,128)(2,1)S(1)}, bf16[3,2,512,1024]{3,2,1,0:T(8,128)(2,1)}, u32[]{:S(2)}) copy-start(bf16[3,2,512,1024]{3,2,1,0:T(8,128)(2,1)} %shard_map.74) | copy-start | bytes 18874372
  73.8 11.4 %all-to-all-start.1 = ((bf16[16,32,128]{2,1,0:T(8,128)(2,1)}), bf16[16,32,128]{2,1,0:T(8,128)(2,1)S(1)}, u32[]{:S(2)}, u32[]{:S(2)}) async-start(bf16[16,32,128]{2,1,0:T(8,128)(2,1)} %bitcast.10), calls=%async_computation.1 | async-start | bytes 262144 | tf_op jit(solution)/shard_map/all_to_all | solution.py:142
  85.8 1.6 %copy-start.4 = (bf16[1,2,512,1024]{3,2,1,0:T(8,128)(2,1)S(1)}, bf16[1,2,512,1024]{3,2,1,0:T(8,128)(2,1)}, u32[]{:S(2)}) copy-start(bf16[1,2,512,1024]{3,2,1,0:T(8,128)(2,1)} %get-tuple-element.9) | copy-start | bytes 6291460
  88.1 1.6 %copy-start.3 = (bf16[1,2,512,1024]{3,2,1,0:T(8,128)(2,1)S(1)}, bf16[1,2,512,1024]{3,2,1,0:T(8,128)(2,1)}, u32[]{:S(2)}) copy-start(bf16[1,2,512,1024]{3,2,1,0:T(8,128)(2,1)} %get-tuple-element.11) | copy-start | bytes 6291460
  91.4 20.0 %copy-start.8 = (f32[256]{0:T(256)S(1)}, f32[256]{0:T(256)}, u32[]{:S(2)}) copy-start(f32[256]{0:T(256)} %param.13) | copy-start | bytes 3076
  104.2 5.8 %collective-permute-start.1 = (bf16[3,256]{1,0:T(4,128)(2,1)S(1)}, bf16[3,256]{1,0:T(4,128)(2,1)S(1)}, u32[]{:S(2)}, u32[]{:S(2)}) collective-permute-start(bf16[3,256]{1,0:T(4,128)(2,1)S(1)} %get-tuple-element.33), channel_id=1, source_target_pairs={{1,0},{3,2},{5,4},{7,6},{9,8},{11,10},{13,12},{15,14},{17,16},{19,... | collective-permute-start | bytes 4616 | tf_op jit(solution)/shard_map/ppermute | solution.py:163
  105.5 5.8 %collective-permute-start = (bf16[3,256]{1,0:T(4,128)(2,1)S(1)}, bf16[3,256]{1,0:T(4,128)(2,1)S(1)}, u32[]{:S(2)}, u32[]{:S(2)}) collective-permute-start(bf16[3,256]{1,0:T(4,128)(2,1)S(1)} %get-tuple-element.32), channel_id=1, source_target_pairs={{0,1},{2,3},{4,5},{6,7},{8,9},{10,11},{12,13},{14,15},{16,17},{18,... | collective-permute-start | bytes 4616 | tf_op jit(solution)/shard_map/ppermute | solution.py:162
Sparse Core Ops, SparseCore 0:
  19.0 50.7 all-gather.2
where the time goes:
time: 121 us; the launch traced here: 120 us
  blocking collectives  29.3 us (24%)
  waiting for transfers between devices  25.6 us (21%)
  local copies, waits for them, and re-layouts  15.7 us (13%)
  between operations  13.9 us (11%)
  Pallas kernels  13.2 us (11%)
  matrix products  10.5 us (9%)
  starting transfers between devices  9.33 us (8%)
  other arithmetic  2.48 us (2%)
    all_gather x1, waiting for transfers between devices, local(): filt = lax.all_gather(part, 'sub', axis=1, tiled=True)  18.1 us
    pallas_call x2, Pallas kernels, merge_operators(): pl.pallas_call(operator_body, grid=(levels, 2, 2), in_specs=[pl.BlockSpec...  13.2 us
    all_to_all x1, blocking collectives, local(): lax.all_to_all(power, 'sub', split_axis=0, concat_axis=0, tiled=True)  12.6 us
    dot_general x12, matrix products, low_dot(): return jnp.dot(left, right, preferred_element_type=jnp.float32)  9.98 us
    all_to_all x1, blocking collectives, local(): lax.all_to_all(range_filter, 'chan', split_axis=2, concat_axis=1, tiled=T...  9.24 us
    all_gather x1, blocking collectives, local(): echo = lax.all_gather(raw_pulses[:, :, 0, :], 'chan', axis=0)  7.41 us
    unnamed x25, local copies, waits for them, and re-layouts  6.64 us
    all_to_all x1, waiting for transfers between devices, local(): got = lax.all_to_all(blocks, 'sub', split_axis=0, concat_axis=0, tiled=True)  6.19 us
  transfers between devices with their start and end apart: 4, of which 3 were waited for; matrix products, arithmetic and copies ran while one was open for 10% of the time, Pallas kernels for 11%

commit v1 on v0

--- a/solution.py
+++ b/solution.py
@@ -1,15 +1,19 @@
+import functools
+
 import jax
 import jax.numpy as jnp
 import numpy as np
 from jax import lax
 from jax.experimental import pallas as pl
+from jax.experimental.pallas import tpu as pltpu
 from jax.sharding import PartitionSpec as P
 
 PASSES = 3
+HALO = 16
+LANES = 128
 HIGH = lax.Precision.HIGHEST
 LOW = jnp.bfloat16
-
-
+MESH = pl.DeviceIdType.MESH
 def rounded(value):
     return lax.reduce_precision(value, exponent_bits=8, mantissa_bits=7)
 
@@ -108,7 +112,7 @@
     return jnp.dot(left, right, preferred_element_type=jnp.float32)
 
 
-def local(
+def local_plain(
     raw_pulses, range_filter, channel_mix, steer_angles, band_offsets, band_weights, smoothing
 ):
     pulses = raw_pulses.shape[1]
@@ -177,6 +181,532 @@
     return power.T
 
 
+def flip(value, bits):
+    out = value
+    step = 1
+    while step <= bits:
+        if bits & step:
+            out = out + step - 2 * step * ((value // step) % 2)
+        step *= 2
+    return out
+
+
+def forming_rows(channel_mix, steer_angles, pulse_count):
+    channels = channel_mix.shape[2]
+    dop_r, dop_i = doppler_table(pulse_count)
+    beam_r, beam_i = steer_table(steer_angles, channels * pulse_count)
+    mix = channel_mix.transpose(0, 3, 2, 1)[:, :, None, :, :]
+    dr, di = dop_r.T[None, :, None, :], dop_i.T[None, :, None, :]
+    shape = (channels * pulse_count, channels * pulse_count)
+    mixed_r = (mix[0] * dr - mix[1] * di).reshape(shape)
+    mixed_i = (mix[0] * di + mix[1] * dr).reshape(shape)
+    left = jnp.concatenate([mixed_r, mixed_i], axis=1)
+    t_r = jnp.dot(left, jnp.concatenate([beam_r, -beam_i], axis=0), precision=HIGH)
+    t_i = jnp.dot(left, jnp.concatenate([beam_i, beam_r], axis=0), precision=HIGH)
+    top = jnp.concatenate([t_r, t_i], axis=1)
+    low = jnp.concatenate([-t_i, t_r], axis=1)
+    return jnp.concatenate([top, low], axis=0)
+
+
+def window_body(
+    subs,
+    filt_hbm,
+    raw_hbm,
+    form_ref,
+    offs_ref,
+    wts_ref,
+    out_ref,
+    bsrc,
+    ys,
+    bg,
+    echo,
+    acc,
+    base_hi,
+    base_lo,
+    fold_hi,
+    fold_lo,
+    ops,
+    sbuf,
+    img0,
+    img_a,
+    img_b,
+    pbuf,
+    rows_c,
+    loc_sem,
+    y_s,
+    y_r,
+    bz_s,
+    bz_r,
+    bx_s,
+    bx_r,
+    a_s,
+    a_r,
+    sb_s,
+    sb_r,
+    sc_s,
+    sc_r,
+    h_s,
+    h_r,
+):
+    chans = 2
+    rows = bsrc.shape[1]
+    half = ys.shape[2]
+    pulses = echo.shape[3]
+    own = img0.shape[2]
+    angles = form_ref.shape[1] // 2
+    depth = subs // 4
+    group = subs // 4
+    levels = offs_ref.shape[0]
+
+    s, c = lax.axis_index("sub"), lax.axis_index("chan")
+    z, x, k = s // 4, (s // 2) % 2, s % 2
+    par, zp = z % 2, z // 2
+
+    def sub_at(dz, dx, dk):
+        return flip(z, dz) * 4 + flip(x, dx) * 2 + flip(k, dk)
+
+    def device(dz, dx, dk, dc):
+        return {"sub": sub_at(dz, dx, dk), "chan": flip(c, dc)}
+
+    def remote(src, dst, send, recv, dev):
+        return pltpu.make_async_remote_copy(
+            src_ref=src, dst_ref=dst, send_sem=send, recv_sem=recv, device_id=dev, device_id_type=MESH
+        )
+
+    q_me = par * 2 + k
+    load_b = pltpu.make_async_copy(filt_hbm, bsrc, loc_sem.at[0])
+    load_a = pltpu.make_async_copy(raw_hbm, echo.at[q_me, :, c], loc_sem.at[1])
+    load_b.start()
+    load_a.start()
+
+    barrier = pltpu.get_barrier_semaphore()
+    greeted = [(0, 0, 0, 1), (0, 1, 0, 0)]
+    greeted += [(dz, 0, dk, 0) for dz in range(depth) for dk in range(2) if dz or dk]
+    for who in greeted:
+        pl.semaphore_signal(barrier, inc=1, device_id=device(*who), device_id_type=MESH)
+    pl.semaphore_wait(barrier, len(greeted))
+
+    sent = []
+
+    def go(copy):
+        copy.start()
+        sent.append(copy)
+
+    def spot(dz, dx, dk, dc):
+        at = (sub_at(dz, dx, dk) * chans + flip(c, dc)) * rows
+        return bg.at[:, pl.ds(pl.multiple_of(at, rows), rows), :]
+
+    def column(dz, dk):
+        return ((flip(z, dz) % 2) * 2 + flip(k, dk)) * LANES
+
+    def piece(dz, dk, dc):
+        if dc:
+            return ys.at[:, :, pl.ds(pl.multiple_of(column(dz, dk), LANES), LANES)]
+        at = c * half + column(dz, dk)
+        return bsrc.at[:, :, pl.ds(pl.multiple_of(at, LANES), LANES)]
+
+    def block(dz, dk, dc):
+        return remote(
+            piece(dz, dk, dc), spot(0, 0, 0, dc), bz_s.at[dz, dk, dc], bz_r.at[dz, dk, dc], device(dz, 0, dk, 0)
+        )
+
+    def arrived(dz, dk, dc):
+        remote(
+            piece(dz, dk, dc), spot(dz, 0, dk, dc), bz_s.at[dz, dk, dc], bz_r.at[dz, dk, dc], device(dz, 0, dk, 0)
+        ).wait_recv()
+
+    def across(dz, dk, dc):
+        return remote(
+            spot(dz, 0, dk, dc), spot(dz, 0, dk, dc), bx_s.at[dz, dk, dc], bx_r.at[dz, dk, dc], device(0, 1, 0, 0)
+        )
+
+    def crossed(dz, dk, dc):
+        remote(
+            spot(dz, 1, dk, dc), spot(dz, 1, dk, dc), bx_s.at[dz, dk, dc], bx_r.at[dz, dk, dc], device(0, 1, 0, 0)
+        ).wait_recv()
+
+    def echo_at(da, dk, dc):
+        return echo.at[flip(par, da) * 2 + flip(k, dk), :, flip(c, dc)]
+
+    def pass_echo(slot, here, there, dev):
+        spot_here = echo_at(*here)
+        go(remote(spot_here, spot_here, a_s.at[slot], a_r.at[there[0], there[1], there[2]], device(*dev)))
+
+    def echo_in(da, dk, dc):
+        there = echo_at(da, dk, dc)
+        remote(there, there, a_s.at[0], a_r.at[da, dk, dc], device(0, 0, 0, 1)).wait_recv()
+
+    def build(level, side):
+        block_rows = 32
+        lane = side * angles
+        offs = offs_ref[level, :, lane : lane + angles]
+
+        def strip(i, carry):
+            at = pl.multiple_of(i * block_rows, block_rows)
+            delta = lax.broadcasted_iota(jnp.int32, (block_rows, angles), 0) + at - offs
+            band = [[jnp.zeros((block_rows, angles), jnp.float32)] * 2 for _ in range(2)]
+            for j in range(wts_ref.shape[3]):
+                hit = delta == j
+                for child in range(2):
+                    for part in range(2):
+                        row = wts_ref[level, child, part, j : j + 1, lane : lane + angles]
+                        band[child][part] = jnp.where(hit, row, band[child][part])
+            left = 2 * lane
+            for child in range(2):
+                real, imag = band[child]
+                for order in range(2 if level == 0 else 1):
+                    r, m = real.astype(LOW), imag.astype(LOW)
+                    if level == 0:
+                        ref = (base_hi if order == 0 else base_lo).at[child]
+                    else:
+                        ref = ops.at[level - 1, child]
+                    low = pl.ds(pl.multiple_of(angles + at, block_rows), block_rows)
+                    ref[pl.ds(at, block_rows), left : left + angles] = r
+                    ref[pl.ds(at, block_rows), left + angles : left + 2 * angles] = m
+                    ref[low, left : left + angles] = -m
+                    ref[low, left + angles : left + 2 * angles] = r
+                    real, imag = real - r.astype(jnp.float32), imag - m.astype(jnp.float32)
+            return carry
+
+        lax.fori_loop(0, angles // block_rows, strip, 0)
+
+    def fold():
+        form = form_ref[...]
+        top = form.astype(LOW)
+        low = (form - top.astype(jnp.float32)).astype(LOW)
+        feats = form.shape[0]
+        for child in range(2):
+            hi, lo = base_hi[child], base_lo[child]
+            value = low_dot(top, hi) + (low_dot(low, hi) + low_dot(top, lo))
+            first = value.astype(LOW)
+            at = slice(child * feats, (child + 1) * feats)
+            fold_hi[at, :] = first
+            fold_lo[at, :] = (value - first.astype(jnp.float32)).astype(LOW)
+
+    def multiply(dz, dx, fresh):
+        pair = flip(z, dz) * 2 + flip(x, dx)
+        wide = 2 * chans * rows
+        at = pl.multiple_of(pair * wide, wide)
+        left = echo[:, :, :, :, pl.ds(at, wide)].reshape(-1, wide)
+        right = jnp.concatenate([bg[0, pl.ds(at, wide), :], bg[1, pl.ds(at, wide), :]], axis=1)
+        value = low_dot(left, right)
+        acc[...] = value if fresh else acc[...] + value
+
+    load_b.wait()
+    other = pl.multiple_of((1 - c) * half, half)
+    go(remote(bsrc.at[:, :, pl.ds(other, half)], ys, y_s, y_r, device(0, 0, 0, 1)))
+    keep = pltpu.make_async_copy(piece(0, 0, 0), spot(0, 0, 0, 0), bz_r.at[0, 0, 0])
+    keep.start()
+    go(block(0, 1, 0))
+    load_a.wait()
+    pass_echo(0, (0, 0, 0), (1, 0, 0), (1, 0, 0, 0))
+    pass_echo(1, (0, 0, 0), (0, 0, 1), (0, 0, 0, 1))
+    far = [dz for dz in range(depth - 1, 0, -1)]
+    for dz in far:
+        for dk in range(2):
+            go(block(dz, dk, 0))
+    pass_echo(2, (0, 0, 0), (0, 1, 0), (0, 0, 1, 0))
+    keep.wait()
+    go(across(0, 0, 0))
+    build(0, 0)
+    arrived(0, 1, 0)
+    go(across(0, 1, 0))
+    build(0, 1)
+
+    remote(ys, ys, y_s, y_r, device(0, 0, 0, 1)).wait_recv()
+    keep = pltpu.make_async_copy(piece(0, 0, 1), spot(0, 0, 0, 1), bz_r.at[0, 0, 1])
+    keep.start()
+    go(block(0, 1, 1))
+    for dz in far:
+        for dk in range(2):
+            go(block(dz, dk, 1))
+    keep.wait()
+    go(across(0, 0, 1))
+    fold()
+    arrived(0, 1, 1)
+    go(across(0, 1, 1))
+
+    pending = [(level, side) for level in range(1, levels) for side in range(2)]
+    echo_in(1, 0, 0)
+    pass_echo(3, (1, 0, 0), (1, 0, 1), (0, 0, 0, 1))
+    pass_echo(4, (1, 0, 0), (1, 1, 0), (0, 0, 1, 0))
+    for dz in far:
+        for dk in range(2):
+            arrived(dz, dk, 0)
+            go(across(dz, dk, 0))
+        if pending:
+            build(*pending.pop(0))
+    echo_in(0, 0, 1)
+    pass_echo(5, (0, 0, 1), (0, 1, 1), (0, 0, 1, 0))
+    for dz in far:
+        for dk in range(2):
+            arrived(dz, dk, 1)
+            go(across(dz, dk, 1))
+        if pending:
+            build(*pending.pop(0))
+    while pending:
+        build(*pending.pop(0))
+    echo_in(1, 0, 1)
+    pass_echo(6, (1, 0, 1), (1, 1, 1), (0, 0, 1, 0))
+    for da in range(2):
+        for dc in range(2):
+            echo_in(da, 1, dc)
+    multiply(0, 0, True)
+    for dz in far:
+        multiply(dz, 0, False)
+    for dz in [0] + far:
+        for dk in range(2):
+            for dc in range(2):
+                crossed(dz, dk, dc)
+        multiply(dz, 1, False)
+
+    feats = form_ref.shape[0]
+    value = acc[...].reshape(4, 2, feats // 2, 2 * LANES)
+    for q in range(4):
+        real = value[q, 0, :, :LANES] - value[q, 1, :, LANES:]
+        imag = value[q, 0, :, LANES:] + value[q, 1, :, :LANES]
+        turned = jnp.concatenate([real, imag], axis=0).T.astype(LOW)
+        sbuf[:, q] = turned.reshape(group, own, feats)
+    mine = zp * 2 + x
+    spread = [(dzp, dx) for dzp in range(depth // 2 - 1, -1, -1) for dx in (1, 0)]
+    for dzp, dx in spread:
+        slot = dzp * 2 + dx
+        if slot:
+            to = flip(zp, dzp) * 2 + flip(x, dx)
+            go(remote(sbuf.at[to], img0.at[mine], sb_s.at[slot], sb_r.at[slot], device(2 * dzp, dx, 0, 0)))
+    img0[mine] = sbuf[mine]
+    for dzp, dx in spread:
+        slot = dzp * 2 + dx
+        if slot:
+            origin = flip(zp, dzp) * 2 + flip(x, dx)
+            remote(
+                sbuf.at[origin], img0.at[origin], sb_s.at[slot], sb_r.at[slot], device(2 * dzp, dx, 0, 0)
+            ).wait_recv()
+
+    place = (depth // 2, 2, 2, 2)
+    wide = 2 * angles
+
+    def child_rows(ref, axis, child, cols):
+        split = (place[0] // 2, 2) + place[1:] if axis == 0 else place
+        at = 1 if axis == 0 else axis
+        whole = ref[...].reshape(split + (own, cols))
+        return lax.index_in_dim(whole, child, at, keepdims=False).reshape(-1, cols)
+
+    axis_of = [3, 1, 2] + [0] * (levels - 3)
+    pair = jnp.concatenate([child_rows(img0, 3, child, feats) for child in range(2)], axis=1)
+    source, target = img_a, img_b
+    for side in range(2):
+        cols = slice(side * wide, (side + 1) * wide)
+        out = low_dot(pair, fold_hi[:, cols]) + low_dot(pair, fold_lo[:, cols])
+        source[:, :, :, side] = out.astype(LOW).reshape(place[:3] + (own, wide))
+    for level in range(1, levels - 1):
+        first, second = (child_rows(source, axis_of[level], child, wide) for child in range(2))
+        for side in range(2):
+            cols = slice(side * wide, (side + 1) * wide)
+            out = low_dot(first, ops[level - 1, 0, :, cols]) + low_dot(second, ops[level - 1, 1, :, cols])
+            out = out.astype(LOW)
+            if axis_of[level] == 1:
+                target[:, side] = out.reshape(place[0], 2, 2, own, wide)
+            else:
+                target[:, :, side] = out.reshape(place[0], 2, 2, own, wide)
+        source, target = target, source
+    first, second = (child_rows(source, 0, child, wide) for child in range(2))
+    base = HALO + (q_me * group + mine) * own
+    block_at = pl.multiple_of(base, HALO)
+
+    for turn in (1, 0):
+        side = flip(zp, turn) % 2
+        cols = pl.ds(pl.multiple_of(side * wide, wide), wide)
+        out = low_dot(first, ops[levels - 2, 0, :, cols]) + low_dot(second, ops[levels - 2, 1, :, cols])
+        power = out[:, :angles] * out[:, :angles] + out[:, angles:] * out[:, angles:]
+        power = power.astype(LOW).reshape(place[0] // 2, 2, 2, 2, own, angles)
+        for pair_at in range(place[0] // 2):
+            pbuf[pair_at * 2 + side] = power[pair_at]
+        for high in range(place[0] // 2):
+            dzp = high * 2 + turn
+            for rel in range(8):
+                dx, dzz, dk = rel // 4, (rel // 2) % 2, rel % 2
+                slot = dzp * 8 + rel
+                src = pbuf.at[flip(zp, dzp), flip(x, dx), flip(par, dzz), flip(k, dk)]
+                if slot:
+                    go(
+                        remote(
+                            src,
+                            rows_c.at[pl.ds(block_at, own), :],
+                            sc_s.at[slot],
+                            sc_r.at[slot],
+                            device(2 * dzp + dzz, dx, dk, 0),
+                        )
+                    )
+
+    def halo(slot, up):
+        dzp, rel = slot // 8, slot % 8
+        dx, dzz, dk = rel // 4, (rel // 2) % 2, rel % 2
+        src = pbuf.at[flip(zp, dzp), flip(x, dx), flip(par, dzz), flip(k, dk)]
+        src = src.at[pl.ds(own - HALO if up else 0, HALO), :]
+        dst = rows_c.at[pl.ds(0 if up else HALO + half, HALO), :]
+        return remote(src, dst, h_s.at[slot], h_r.at[0 if up else 1], device(2 * dzp + dzz, dx, dk, 1))
+
+    order = list(range(subs - 1, -1, -1))
+    sends_up = jnp.logical_and(c == 0, base == HALO + half - own)
+    sends_down = jnp.logical_and(c == 1, base == HALO)
+
+    @pl.when(sends_up)
+    def _():
+        for slot in order:
+            halo(slot, True).start()
+
+    @pl.when(sends_down)
+    def _():
+        for slot in order:
+            halo(slot, False).start()
+
+    rows_c[pl.ds(block_at, own), :] = pbuf[zp, x, par, k]
+
+    @pl.when(c == 0)
+    def _():
+        rows_c[pl.ds(0, HALO), :] = jnp.zeros((HALO, angles), LOW)
+
+    @pl.when(c == 1)
+    def _():
+        rows_c[pl.ds(HALO + half, HALO), :] = jnp.zeros((HALO, angles), LOW)
+
+    for slot in order:
+        if slot:
+            dzp, rel = slot // 8, slot % 8
+            dx, dzz, dk = rel // 4, (rel // 2) % 2, rel % 2
+            origin = (flip(par, dzz) * 2 + flip(k, dk)) * group + flip(zp, dzp) * 2 + flip(x, dx)
+            at = pl.multiple_of(HALO + origin * own, HALO)
+            dst = rows_c.at[pl.ds(at, own), :]
+            remote(
+                dst, dst, sc_s.at[slot], sc_r.at[slot], device(2 * dzp + dzz, dx, dk, 0)
+            ).wait_recv()
+
+    @pl.when(c == 1)
+    def _():
+        halo(0, True).wait_recv()
+
+    @pl.when(c == 0)
+    def _():
+        halo(0, False).wait_recv()
+
+    out_ref[...] = rows_c[...]
+
+    for copy in sent:
+        copy.wait_send()
+
+    @pl.when(sends_up)
+    def _():
+        for slot in order:
+            halo(slot, True).wait_send()
+
+    @pl.when(sends_down)
+    def _():
+        for slot in order:
+            halo(slot, False).wait_send()
+
+
+def smooth_body(chans, power_ref, rate_ref, out_ref):
+    at = lax.axis_index("chan")
+    power = power_ref[...].astype(jnp.float32)
+    rate = rate_ref[...]
+    height = power.shape[0] - 2 * HALO
+    row = lax.broadcasted_iota(jnp.int32, power.shape, 0)
+    inside = jnp.logical_and(
+        jnp.logical_or(row >= HALO, at > 0), jnp.logical_or(row < HALO + height, at < chans - 1)
+    )
+    for sweep in range(PASSES):
+        before = jnp.concatenate([power[:1], power[:-1]], axis=0)
+        after = jnp.concatenate([power[1:], power[-1:]], axis=0)
+        power = power + rate * (before - 2.0 * power + after)
+        power = jnp.where(inside, power, 0.0)
+    out_ref[...] = power[HALO : HALO + height].T
+
+
+def local_kernel(
+    raw_pulses, range_filter, channel_mix, steer_angles, band_offsets, band_weights, smoothing
+):
+    _, pulses, _, samples = raw_pulses.shape
+    _, rows, bins = range_filter.shape
+    angles = steer_angles.shape[0]
+    levels, _, _, merged, band_width = band_weights.shape
+    subs, chans = lax.axis_size("sub"), lax.axis_size("chan")
+    half = bins // chans
+    group = subs // 4
+    own = LANES // group
+    depth = subs // 4
+    feats = 2 * chans * pulses
+    form = forming_rows(channel_mix, steer_angles, pulses)
+    place = (depth // 2, 2, 2, 2)
+    dma = pltpu.SemaphoreType.DMA
+    vmem = pl.BlockSpec(memory_space=pltpu.VMEM)
+    anywhere = pl.BlockSpec(memory_space=pl.ANY)
+    power = pl.pallas_call(
+        functools.partial(window_body, subs),
+        out_shape=jax.ShapeDtypeStruct((half + 2 * HALO, angles), LOW),
+        in_specs=[anywhere, anywhere, vmem, vmem, vmem],
+        out_specs=vmem,
+        scratch_shapes=[
+            pltpu.VMEM((2, rows, bins), LOW),
+            pltpu.VMEM((2, rows, half), LOW),
+            pltpu.VMEM((2, subs * chans * rows, LANES), LOW),
+            pltpu.VMEM((4, 2, chans, pulses, samples), LOW),
+            pltpu.VMEM((4 * feats, 2 * LANES), jnp.float32),
+            pltpu.VMEM((2, 2 * angles, 2 * merged), LOW),
+            pltpu.VMEM((2, 2 * angles, 2 * merged), LOW),
+            pltpu.VMEM((2 * feats, 2 * merged), LOW),
+            pltpu.VMEM((2 * feats, 2 * merged), LOW),
+            pltpu.VMEM((levels - 1, 2, 2 * angles, 2 * merged), LOW),
+            pltpu.VMEM((group, 4, own, feats), LOW),
+            pltpu.VMEM((group, 4, own, feats), LOW),
+            pltpu.VMEM(place + (own, 2 * angles), LOW),
+            pltpu.VMEM(place + (own, 2 * angles), LOW),
+            pltpu.VMEM(place + (own, angles), LOW),
+            pltpu.VMEM((half + 2 * HALO, angles), LOW),
+            dma((2,)),
+            dma,
+            dma,
+            dma((depth, 2, 2)),
+            dma((depth, 2, 2)),
+            dma((depth, 2, 2)),
+            dma((depth, 2, 2)),
+            dma((7,)),
+            dma((2, 2, 2)),
+            dma((group,)),
+            dma((group,)),
+            dma((subs,)),
+            dma((subs,)),
+            dma((subs,)),
+            dma((2,)),
+        ],
+        compiler_params=pltpu.CompilerParams(
+            collective_id=0, has_side_effects=True, vmem_limit_bytes=56 << 20
+        ),
+    )(
+        range_filter,
+        raw_pulses[:, :, 0, :],
+        form,
+        band_offsets[:, None, :],
+        band_weights.transpose(0, 1, 2, 4, 3),
+    )
+    return pl.pallas_call(
+        functools.partial(smooth_body, chans),
+        out_shape=jax.ShapeDtypeStruct((angles, half), jnp.float32),
+        in_specs=[vmem, vmem],
+        out_specs=vmem,
+    )(power, smoothing[None, :])
+
+
+def fits(mesh, raw_pulses, range_filter, steer_angles, band_offsets):
+    subs, chans = mesh.shape["sub"], mesh.shape["chan"]
+    rows = range_filter.shape[1] // (subs * chans)
+    pulses = raw_pulses.shape[1] // subs
+    cut = chans == 2 and subs % 16 == 0 and subs & (subs - 1) == 0
+    cut = cut and range_filter.shape[2] == 4 * chans * LANES and LANES // (subs // 4) >= HALO
+    cut = cut and rows % 16 == 0 and pulses % 16 == 0 and steer_angles.shape[0] % LANES == 0
+    return cut and band_offsets.shape[0] == 4
+
+
 def solution(mesh):
     in_specs = (
         P(None, "sub", "chan", None),
@@ -188,4 +718,12 @@
         P("sub"),
     )
     out_specs = P("sub", "chan")
-    return jax.shard_map(local, mesh=mesh, in_specs=in_specs, out_specs=out_specs, check_vma=False)
+
+    def run(raw_pulses, range_filter, channel_mix, steer_angles, band_offsets, band_weights, smoothing):
+        one = local_kernel if fits(mesh, raw_pulses, range_filter, steer_angles, band_offsets) else local_plain
+        part = jax.shard_map(one, mesh=mesh, in_specs=in_specs, out_specs=out_specs, check_vma=False)
+        return part(
+            raw_pulses, range_filter, channel_mix, steer_angles, band_offsets, band_weights, smoothing
+        )
+
+    return run

time: 121 us -> 50.7 us (0.42)
  Pallas kernels: 13.2 us -> 46 us
  blocking collectives: 29.3 us -> 0 us
  waiting for transfers between devices: 25.6 us -> 0 us
  between operations: 13.9 us -> 0.05 us
  local copies, waits for them, and re-layouts: 15.7 us -> 2.77 us
  matrix products: 10.5 us -> 0.52 us
  starting transfers between devices: 9.33 us -> 0 us
  other arithmetic: 2.48 us -> 1.2 us
    pallas_call x2, Pallas kernels: 13.2 us -> 46 us  [the longest x1 43.6 us: local_kernel(): pl.pallas_call(functools.partial(window_body, subs), out_shape=jax.ShapeD...]
    all_to_all x2 -> x0, blocking collectives: 21.9 us -> none  [the longest x1 12.6 us: local(): lax.all_to_all(power, 'sub', split_axis=0, concat_axis=0, tiled=True)]
    all_gather x1 -> x0, waiting for transfers between devices: 18.1 us -> none  [local(): filt = lax.all_gather(part, 'sub', axis=1, tiled=True)]
    dot_general x14 -> x2, matrix products: 10.5 us -> 0.52 us  [the longest x1 0.26 us: forming_rows(): jnp.dot(left, jnp.concatenate([beam_i, beam_r], axis=0), precision=HIGH)]
    all_gather x1 -> x0, blocking collectives: 7.41 us -> none  [local(): echo = lax.all_gather(raw_pulses[:, :, 0, :], 'chan', axis=0)]
    all_to_all x1 -> x0, waiting for transfers between devices: 6.19 us -> none  [local(): got = lax.all_to_all(blocks, 'sub', split_axis=0, concat_axis=0, tiled=True)]
    ppermute x2 -> x0, starting transfers between devices: 5.82 us -> none  [the longest x1 4.54 us: local(): before = lax.ppermute(power[-PASSES:], 'chan', up).astype(jnp.float32)]
    unnamed x25 -> x6, local copies, waits for them, and re-layouts: 6.64 us -> 1.95 us
  transfers between devices with their start and end apart: 4 -> 0, of which waited for: 3 -> 0; matrix products, arithmetic and copies ran while one was open for 10% -> 0% of each run, Pallas kernels for 11% -> 0%
where the time goes in v1:
time: 50.7 us; the launch traced here: 50.5 us
  Pallas kernels  46 us (91%)
  local copies, waits for them, and re-layouts  2.77 us (5%)
  other arithmetic  1.2 us (2%)
  matrix products  0.52 us (1%)
    pallas_call x1, Pallas kernels, local_kernel(): pl.pallas_call(functools.partial(window_body, subs), out_shape=jax.ShapeD...  43.6 us
    pallas_call x1, Pallas kernels, local_kernel(): pl.pallas_call(functools.partial(smooth_body, chans), out_shape=jax.Shape...  2.32 us
    unnamed x6, local copies, waits for them, and re-layouts  1.95 us

profile of v1, /device:TPU:0, one launch (start us, length us, event | category | flops | bytes accessed | tf_op | source)
XLA Modules:
  0.0 50.5 jit_solution(9670542051096293945)
XLA Ops:
  0.0 0.0 copy-start.1
  0.0 0.7 %copy-done.1 = f32[2,32,2,2]{1,3,2,0:T(2,128)S(1)} copy-done((f32[2,32,2,2]{1,3,2,0:T(2,128)S(1)}, f32[2,32,2,2]{1,3,2,0:T(2,128)}, u32[]{:S(2)}) %copy-start.1) | copy-done | bytes 1048
  0.7 0.0 copy-start
  0.7 0.7 %copy-done = s32[4,512]{1,0:T(4,128)S(1)} copy-done((s32[4,512]{1,0:T(4,128)S(1)}, s32[4,512]{1,0:T(4,128)}, u32[]{:S(2)}) %copy-start) | copy-done | bytes 8216
  1.4 0.6 %broadcast_in_dim.4.offs_ref = s32[4,1,512]{2,1,0:T(1,128)} reshape(s32[4,512]{1,0:T(4,128)S(1)} %copy-done) | data formatting | bytes 16384 | tf_op jit(solution)/shard_map/broadcast_in_dim | solution.py:689
  2.0 0.1 multiply_reduce-precision_fusion
  2.1 0.1 multiply_subtract_fusion
  2.2 0.1 sub.12
  2.3 0.0 copy-start.2
  2.3 0.1 add.35
  2.4 0.6 %copy-done.2 = f32[256]{0:T(256)S(1)} copy-done((f32[256]{0:T(256)S(1)}, f32[256]{0:T(256)}, u32[]{:S(2)}) %copy-start.2) | copy-done | bytes 1048
  2.9 0.3 fusion.11
  3.3 0.3 fusion
  3.5 0.3 fusion.22
  3.8 0.7 %maximum_maximum_fusion.form_ref = f32[128,512]{1,0:T(8,128)} fusion(f32[64,256]{1,0:T(8,128)S(1)} %fusion, f32[64,256]{1,0:T(8,128)S(1)} %get-tuple-element.12, f32[64,256]{1,0:T(8,128)S(1)} %get-tuple-element.13), kind=kLoop, calls=%fused_computation | loop fusion | flops 196608 | bytes 458752 | tf_op jit(solution)/shard_map/concatenate | solution.py:208
  4.5 43.6 %shard_map.73.power_ref = bf16[544,256]{1,0:T(8,128)(2,1)} custom-call(bf16[2,64,1024]{2,1,0:T(8,128)(2,1)} %filt_hbm.1, bf16[2,32,2048]{2,1,0:T(8,128)(2,1)} %bitcast.8, f32[128,512]{1,0:T(8,128)} %maximum_maximum_fusion.form_ref, s32[4,1,512]{2,1,0:T(1,128)} %broadcast_in_dim.4.offs_ref, f32[4,2,2,8,512]{4,3,2,1,0:T(8,128)} %bitcast.9), custom_call_target="tpu_custom_call" | custom-call | tf_op jit(solution)/shard_map/pallas_call | solution.py:644
  48.2 2.3 %shard_map.74 = f32[256,512]{1,0:T(8,128)} custom-call(bf16[544,256]{1,0:T(8,128)(2,1)} %shard_map.73.power_ref, f32[1,256]{1,0:T(1,128)} %bitcast.11), custom_call_target="tpu_custom_call" | custom-call | tf_op jit(solution)/shard_map/pallas_call | solution.py:692
  (3 shorter events, 0.0 us)
Async XLA Ops:
  0.0 0.7 %copy-start.1 = (f32[2,32,2,2]{1,3,2,0:T(2,128)S(1)}, f32[2,32,2,2]{1,3,2,0:T(2,128)}, u32[]{:S(2)}) copy-start(f32[2,32,2,2]{1,3,2,0:T(2,128)} %param.9) | copy-start | bytes 3076
  0.7 0.7 %copy-start = (s32[4,512]{1,0:T(4,128)S(1)}, s32[4,512]{1,0:T(4,128)}, u32[]{:S(2)}) copy-start(s32[4,512]{1,0:T(4,128)} %param.11) | copy-start | bytes 24580
  2.3 0.7 %copy-start.2 = (f32[256]{0:T(256)S(1)}, f32[256]{0:T(256)}, u32[]{:S(2)}) copy-start(f32[256]{0:T(256)} %param.10) | copy-start | bytes 3076

commit v2 on v1

--- a/solution.py
+++ b/solution.py
@@ -181,6 +181,14 @@
     return power.T
 
 
+def narrow(value):
+    return value.astype(LOW).astype(jnp.float32)
+
+
+def high_dot(left, right):
+    return jnp.dot(left, right, precision=HIGH, preferred_element_type=jnp.float32)
+
+
 def flip(value, bits):
     out = value
     step = 1
@@ -191,18 +199,34 @@
     return out
 
 
-def forming_rows(channel_mix, steer_angles, pulse_count):
-    channels = channel_mix.shape[2]
-    dop_r, dop_i = doppler_table(pulse_count)
-    beam_r, beam_i = steer_table(steer_angles, channels * pulse_count)
-    mix = channel_mix.transpose(0, 3, 2, 1)[:, :, None, :, :]
-    dr, di = dop_r.T[None, :, None, :], dop_i.T[None, :, None, :]
-    shape = (channels * pulse_count, channels * pulse_count)
-    mixed_r = (mix[0] * dr - mix[1] * di).reshape(shape)
-    mixed_i = (mix[0] * di + mix[1] * dr).reshape(shape)
-    left = jnp.concatenate([mixed_r, mixed_i], axis=1)
-    t_r = jnp.dot(left, jnp.concatenate([beam_r, -beam_i], axis=0), precision=HIGH)
-    t_i = jnp.dot(left, jnp.concatenate([beam_i, beam_r], axis=0), precision=HIGH)
+def forming_rows(mix_ref, steer, pulse_count):
+    bands, channels = mix_ref.shape[1], mix_ref.shape[2]
+    angles = steer.shape[1]
+    square = (pulse_count, pulse_count)
+    product = lax.broadcasted_iota(jnp.int32, square, 0) * lax.broadcasted_iota(jnp.int32, square, 1)
+    product = product.astype(jnp.float32)
+    product = product - pulse_count * jnp.floor(product / pulse_count)
+    phase = 2.0 * np.pi / pulse_count * product
+    factor = 1.0 / np.sqrt(pulse_count)
+    dop_r, dop_i = narrow(jnp.cos(phase) * factor), narrow(-jnp.sin(phase) * factor)
+    count = channels * pulse_count
+    factor = 1.0 / np.sqrt(count)
+    t_r = t_i = None
+    for band in range(bands):
+        index = lax.broadcasted_iota(jnp.int32, (pulse_count, angles), 0) + band * pulse_count
+        phase = (index.astype(jnp.float32) - 0.5 * count) * steer
+        beam_r, beam_i = narrow(jnp.cos(phase) * factor), narrow(jnp.sin(phase) * factor)
+        mixed = [[], []]
+        for channel in range(channels):
+            mix_r = mix_ref[0, band, channel : channel + 1, :]
+            mix_i = mix_ref[1, band, channel : channel + 1, :]
+            mixed[0].append(mix_r * dop_r - mix_i * dop_i)
+            mixed[1].append(mix_r * dop_i + mix_i * dop_r)
+        mixed_r, mixed_i = (jnp.concatenate(part, axis=0) for part in mixed)
+        add_r = high_dot(mixed_r, beam_r) - high_dot(mixed_i, beam_i)
+        add_i = high_dot(mixed_r, beam_i) + high_dot(mixed_i, beam_r)
+        t_r = add_r if band == 0 else t_r + add_r
+        t_i = add_i if band == 0 else t_i + add_i
     top = jnp.concatenate([t_r, t_i], axis=1)
     low = jnp.concatenate([-t_i, t_r], axis=1)
     return jnp.concatenate([top, low], axis=0)
@@ -212,10 +236,15 @@
     subs,
     filt_hbm,
     raw_hbm,
-    form_ref,
+    mix_hbm,
+    steer_hbm,
+    offs_hbm,
+    wts_hbm,
+    out_ref,
+    mix_ref,
+    steer_ref,
     offs_ref,
     wts_ref,
-    out_ref,
     bsrc,
     ys,
     bg,
@@ -247,13 +276,16 @@
     sc_r,
     h_s,
     h_r,
+    up_sem,
+    down_sem,
 ):
     chans = 2
     rows = bsrc.shape[1]
     half = ys.shape[2]
     pulses = echo.shape[3]
     own = img0.shape[2]
-    angles = form_ref.shape[1] // 2
+    angles = steer_ref.shape[1]
+    feats = 2 * chans * pulses
     depth = subs // 4
     group = subs // 4
     levels = offs_ref.shape[0]
@@ -276,15 +308,61 @@
     q_me = par * 2 + k
     load_b = pltpu.make_async_copy(filt_hbm, bsrc, loc_sem.at[0])
     load_a = pltpu.make_async_copy(raw_hbm, echo.at[q_me, :, c], loc_sem.at[1])
+    tables = [
+        pltpu.make_async_copy(src, dst, loc_sem.at[2 + i])
+        for i, (src, dst) in enumerate(
+            [(offs_hbm, offs_ref), (wts_hbm, wts_ref), (mix_hbm, mix_ref), (steer_hbm, steer_ref)]
+        )
+    ]
     load_b.start()
     load_a.start()
+    for table in tables:
+        table.start()
 
     barrier = pltpu.get_barrier_semaphore()
-    greeted = [(0, 0, 0, 1), (0, 1, 0, 0)]
-    greeted += [(dz, 0, dk, 0) for dz in range(depth) for dk in range(2) if dz or dk]
-    for who in greeted:
-        pl.semaphore_signal(barrier, inc=1, device_id=device(*who), device_id_type=MESH)
-    pl.semaphore_wait(barrier, len(greeted))
+
+    def greet(sub, chan):
+        pl.semaphore_signal(barrier, inc=1, device_id={"sub": sub, "chan": chan}, device_id_type=MESH)
+
+    def along(step, dk):
+        return (z + step) * 4 + x * 2 + flip(k, dk)
+
+    greet(s, 1 - c)
+    greet(sub_at(0, 1, 0), c)
+    greet(sub_at(0, 0, 1), c)
+    below, above = z > 0, z < depth - 1
+
+    @pl.when(below)
+    def _():
+        greet(along(-1, 0), c)
+        greet(along(-1, 1), c)
+
+    @pl.when(above)
+    def _():
+        greet(along(1, 0), c)
+        greet(along(1, 1), c)
+
+    pl.semaphore_wait(barrier, 3 + 2 * lax.min(z, 1) + 2 * lax.min(depth - 1 - z, 1))
+
+    def tell(step, far, sem):
+        pl.semaphore_signal(sem, inc=1, device_id={"sub": along(step, 0), "chan": c}, device_id_type=MESH)
+
+    def spread_word(far):
+        @pl.when(jnp.logical_and(below, z + far - 1 < depth))
+        def _():
+            tell(-1, far, up_sem.at[far - 2])
+
+        @pl.when(jnp.logical_and(above, z - far + 1 >= 0))
+        def _():
+            tell(1, far, down_sem.at[far - 2])
+
+        @pl.when(z + far < depth)
+        def _():
+            pl.semaphore_wait(up_sem.at[far - 2], 1)
+
+        @pl.when(z - far >= 0)
+        def _():
+            pl.semaphore_wait(down_sem.at[far - 2], 1)
 
     sent = []
 
@@ -292,54 +370,67 @@
         copy.start()
         sent.append(copy)
 
-    def spot(dz, dx, dk, dc):
-        at = (sub_at(dz, dx, dk) * chans + flip(c, dc)) * rows
+    inner = (z + zp) % 2
+
+    def reach(turn):
+        if turn == 0:
+            return z, 0
+        if turn == 1:
+            return flip(z, 1), 1
+        if turn == 2:
+            return depth // 2 - zp, 2 + inner
+        return (depth - 1) * (1 - zp), 3 - inner
+
+    def spot(at_z, dx, dk, dc):
+        at = ((at_z * 4 + flip(x, dx) * 2 + flip(k, dk)) * chans + flip(c, dc)) * rows
         return bg.at[:, pl.ds(pl.multiple_of(at, rows), rows), :]
 
-    def column(dz, dk):
-        return ((flip(z, dz) % 2) * 2 + flip(k, dk)) * LANES
-
-    def piece(dz, dk, dc):
+    def piece(at_z, dk, dc):
+        column = ((at_z % 2) * 2 + flip(k, dk)) * LANES
         if dc:
-            return ys.at[:, :, pl.ds(pl.multiple_of(column(dz, dk), LANES), LANES)]
-        at = c * half + column(dz, dk)
-        return bsrc.at[:, :, pl.ds(pl.multiple_of(at, LANES), LANES)]
-
-    def block(dz, dk, dc):
-        return remote(
-            piece(dz, dk, dc), spot(0, 0, 0, dc), bz_s.at[dz, dk, dc], bz_r.at[dz, dk, dc], device(dz, 0, dk, 0)
-        )
-
-    def arrived(dz, dk, dc):
-        remote(
-            piece(dz, dk, dc), spot(dz, 0, dk, dc), bz_s.at[dz, dk, dc], bz_r.at[dz, dk, dc], device(dz, 0, dk, 0)
-        ).wait_recv()
-
-    def across(dz, dk, dc):
-        return remote(
-            spot(dz, 0, dk, dc), spot(dz, 0, dk, dc), bx_s.at[dz, dk, dc], bx_r.at[dz, dk, dc], device(0, 1, 0, 0)
-        )
-
-    def crossed(dz, dk, dc):
-        remote(
-            spot(dz, 1, dk, dc), spot(dz, 1, dk, dc), bx_s.at[dz, dk, dc], bx_r.at[dz, dk, dc], device(0, 1, 0, 0)
-        ).wait_recv()
-
-    def echo_at(da, dk, dc):
-        return echo.at[flip(par, da) * 2 + flip(k, dk), :, flip(c, dc)]
-
-    def pass_echo(slot, here, there, dev):
-        spot_here = echo_at(*here)
-        go(remote(spot_here, spot_here, a_s.at[slot], a_r.at[there[0], there[1], there[2]], device(*dev)))
-
-    def echo_in(da, dk, dc):
-        there = echo_at(da, dk, dc)
-        remote(there, there, a_s.at[0], a_r.at[da, dk, dc], device(0, 0, 0, 1)).wait_recv()
+            return ys.at[:, :, pl.ds(pl.multiple_of(column, LANES), LANES)]
+        return bsrc.at[:, :, pl.ds(pl.multiple_of(c * half + column, LANES), LANES)]
+
+    def block(turn, dk, dc):
+        at_z, bits = reach(turn)
+        to = {"sub": at_z * 4 + x * 2 + flip(k, dk), "chan": c}
+        return remote(piece(at_z, dk, dc), spot(z, 0, 0, dc), bz_s.at[turn, dk, dc], bz_r.at[bits, dk, dc], to)
+
+    def keep(dc):
+        copy = pltpu.make_async_copy(piece(z, 0, dc), spot(z, 0, 0, dc), bz_r.at[0, 0, dc])
+        copy.start()
+        return copy
+
+    def arrived(turn, dk, dc):
+        at_z, bits = reach(turn)
+        here = spot(at_z, 0, dk, dc)
+        remote(here, here, bz_s.at[turn, dk, dc], bz_r.at[bits, dk, dc], device(0, 1, 0, 0)).wait_recv()
+
+    def across(turn, dk, dc):
+        at_z, bits = reach(turn)
+        here = spot(at_z, 0, dk, dc)
+        return remote(here, here, bx_s.at[turn, dk, dc], bx_r.at[bits, dk, dc], device(0, 1, 0, 0))
+
+    def crossed(turn, dk, dc):
+        at_z, bits = reach(turn)
+        there = spot(at_z, 1, dk, dc)
+        remote(there, there, bx_s.at[turn, dk, dc], bx_r.at[bits, dk, dc], device(0, 1, 0, 0)).wait_recv()
+
+    def echo_at(da, dk, dc, part):
+        return echo.at[flip(par, da) * 2 + flip(k, dk), part, flip(c, dc)]
+
+    def pass_echo(slot, here, there, dev, part):
+        spot_here = echo_at(*here, part)
+        go(remote(spot_here, spot_here, a_s.at[slot, part], a_r.at[there + (part,)], device(*dev)))
+
+    def echo_in(da, dk, dc, part):
+        there = echo_at(da, dk, dc, part)
+        remote(there, there, a_s.at[0, part], a_r.at[da, dk, dc, part], device(0, 0, 0, 1)).wait_recv()
 
     def build(level, side):
         block_rows = 32
         lane = side * angles
-        offs = offs_ref[level, :, lane : lane + angles]
+        offs = offs_ref[level : level + 1, lane : lane + angles]
 
         def strip(i, carry):
             at = pl.multiple_of(i * block_rows, block_rows)
@@ -371,10 +462,9 @@
         lax.fori_loop(0, angles // block_rows, strip, 0)
 
     def fold():
-        form = form_ref[...]
+        form = forming_rows(mix_ref, steer_ref[...], pulses)
         top = form.astype(LOW)
         low = (form - top.astype(jnp.float32)).astype(LOW)
-        feats = form.shape[0]
         for child in range(2):
             hi, lo = base_hi[child], base_lo[child]
             value = low_dot(top, hi) + (low_dot(low, hi) + low_dot(top, lo))
@@ -383,8 +473,8 @@
             fold_hi[at, :] = first
             fold_lo[at, :] = (value - first.astype(jnp.float32)).astype(LOW)
 
-    def multiply(dz, dx, fresh):
-        pair = flip(z, dz) * 2 + flip(x, dx)
+    def multiply(turn, dx, fresh):
+        pair = reach(turn)[0] * 2 + flip(x, dx)
         wide = 2 * chans * rows
         at = pl.multiple_of(pair * wide, wide)
         left = echo[:, :, :, :, pl.ds(at, wide)].reshape(-1, wide)
@@ -395,72 +485,102 @@
     load_b.wait()
     other = pl.multiple_of((1 - c) * half, half)
     go(remote(bsrc.at[:, :, pl.ds(other, half)], ys, y_s, y_r, device(0, 0, 0, 1)))
-    keep = pltpu.make_async_copy(piece(0, 0, 0), spot(0, 0, 0, 0), bz_r.at[0, 0, 0])
-    keep.start()
+    kept = keep(0)
     go(block(0, 1, 0))
     load_a.wait()
-    pass_echo(0, (0, 0, 0), (1, 0, 0), (1, 0, 0, 0))
-    pass_echo(1, (0, 0, 0), (0, 0, 1), (0, 0, 0, 1))
-    far = [dz for dz in range(depth - 1, 0, -1)]
-    for dz in far:
-        for dk in range(2):
-            go(block(dz, dk, 0))
-    pass_echo(2, (0, 0, 0), (0, 1, 0), (0, 0, 1, 0))
-    keep.wait()
+    pass_echo(0, (0, 0, 0), (1, 0, 0), (1, 0, 0, 0), 0)
+    for part in range(2):
+        pass_echo(1, (0, 0, 0), (0, 0, 1), (0, 0, 0, 1), part)
+    for dk in range(2):
+        go(block(1, dk, 0))
+    for part in range(2):
+        pass_echo(2, (0, 0, 0), (0, 1, 0), (0, 0, 1, 0), part)
+    far_pairs = [block(turn, dk, 0) for turn in range(2, depth) for dk in range(2)]
+    sent.extend(far_pairs)
+
+    @pl.when(inner == 1)
+    def _():
+        for copy in far_pairs[:2]:
+            copy.start()
+
+    kept.wait()
     go(across(0, 0, 0))
-    build(0, 0)
+    spread_word(2)
+
+    @pl.when(inner == 1)
+    def _():
+        for copy in far_pairs[2:]:
+            copy.start()
+
+    @pl.when(inner == 0)
+    def _():
+        for copy in far_pairs[:2]:
+            copy.start()
+
     arrived(0, 1, 0)
     go(across(0, 1, 0))
-    build(0, 1)
+    spread_word(3)
+
+    @pl.when(inner == 0)
+    def _():
+        for copy in far_pairs[2:]:
+            copy.start()
+
+    pass_echo(0, (0, 0, 0), (1, 0, 0), (1, 0, 0, 0), 1)
 
     remote(ys, ys, y_s, y_r, device(0, 0, 0, 1)).wait_recv()
-    keep = pltpu.make_async_copy(piece(0, 0, 1), spot(0, 0, 0, 1), bz_r.at[0, 0, 1])
-    keep.start()
+    kept = keep(1)
     go(block(0, 1, 1))
-    for dz in far:
-        for dk in range(2):
-            go(block(dz, dk, 1))
-    keep.wait()
+    for dk in range(2):
+        for turn in range(1, depth):
+            go(block(turn, dk, 1))
+    kept.wait()
     go(across(0, 0, 1))
-    fold()
+    for table in tables:
+        table.wait()
+    pending = [(level, side) for level in range(levels) for side in range(2)]
+    build(*pending.pop(0))
+
+    def relay(part):
+        echo_in(1, 0, 0, part)
+        pass_echo(3, (1, 0, 0), (1, 0, 1), (0, 0, 0, 1), part)
+        pass_echo(4, (1, 0, 0), (1, 1, 0), (0, 0, 1, 0), part)
+
+    relay(0)
     arrived(0, 1, 1)
     go(across(0, 1, 1))
-
-    pending = [(level, side) for level in range(1, levels) for side in range(2)]
-    echo_in(1, 0, 0)
-    pass_echo(3, (1, 0, 0), (1, 0, 1), (0, 0, 0, 1))
-    pass_echo(4, (1, 0, 0), (1, 1, 0), (0, 0, 1, 0))
-    for dz in far:
+    for dc in range(2):
         for dk in range(2):
-            arrived(dz, dk, 0)
-            go(across(dz, dk, 0))
-        if pending:
-            build(*pending.pop(0))
-    echo_in(0, 0, 1)
-    pass_echo(5, (0, 0, 1), (0, 1, 1), (0, 0, 1, 0))
-    for dz in far:
-        for dk in range(2):
-            arrived(dz, dk, 1)
-            go(across(dz, dk, 1))
-        if pending:
-            build(*pending.pop(0))
+            for turn in range(1, depth):
+                arrived(turn, dk, dc)
+                go(across(turn, dk, dc))
+            if pending:
+                build(*pending.pop(0))
+            if dc == 0 and dk == 1:
+                fold()
+        if dc == 0:
+            relay(1)
+            for part in range(2):
+                echo_in(0, 0, 1, part)
+                pass_echo(5, (0, 0, 1), (0, 1, 1), (0, 0, 1, 0), part)
+    for part in range(2):
+        echo_in(1, 0, 1, part)
+        pass_echo(6, (1, 0, 1), (1, 1, 1), (0, 0, 1, 0), part)
     while pending:
         build(*pending.pop(0))
-    echo_in(1, 0, 1)
-    pass_echo(6, (1, 0, 1), (1, 1, 1), (0, 0, 1, 0))
     for da in range(2):
         for dc in range(2):
-            echo_in(da, 1, dc)
+            for part in range(2):
+                echo_in(da, 1, dc, part)
     multiply(0, 0, True)
-    for dz in far:
-        multiply(dz, 0, False)
-    for dz in [0] + far:
+    for turn in range(1, depth):
+        multiply(turn, 0, False)
+    for turn in range(depth):
         for dk in range(2):
             for dc in range(2):
-                crossed(dz, dk, dc)
-        multiply(dz, 1, False)
-
-    feats = form_ref.shape[0]
+                crossed(turn, dk, dc)
+        multiply(turn, 1, False)
+
     value = acc[...].reshape(4, 2, feats // 2, 2 * LANES)
     for q in range(4):
         real = value[q, 0, :, :LANES] - value[q, 1, :, LANES:]
@@ -636,7 +756,6 @@
     own = LANES // group
     depth = subs // 4
     feats = 2 * chans * pulses
-    form = forming_rows(channel_mix, steer_angles, pulses)
     place = (depth // 2, 2, 2, 2)
     dma = pltpu.SemaphoreType.DMA
     vmem = pl.BlockSpec(memory_space=pltpu.VMEM)
@@ -644,9 +763,13 @@
     power = pl.pallas_call(
         functools.partial(window_body, subs),
         out_shape=jax.ShapeDtypeStruct((half + 2 * HALO, angles), LOW),
-        in_specs=[anywhere, anywhere, vmem, vmem, vmem],
+        in_specs=[pl.BlockSpec(memory_space=pltpu.HBM)] * 6,
         out_specs=vmem,
         scratch_shapes=[
+            pltpu.VMEM((2, chans, chans, pulses), jnp.float32),
+            pltpu.VMEM((1, angles), jnp.float32),
+            pltpu.VMEM((levels, merged), jnp.int32),
+            pltpu.VMEM((levels, 2, 2, band_width, merged), jnp.float32),
             pltpu.VMEM((2, rows, bins), LOW),
             pltpu.VMEM((2, rows, half), LOW),
             pltpu.VMEM((2, subs * chans * rows, LANES), LOW),
@@ -663,37 +786,46 @@
             pltpu.VMEM(place + (own, 2 * angles), LOW),
             pltpu.VMEM(place + (own, angles), LOW),
             pltpu.VMEM((half + 2 * HALO, angles), LOW),
-            dma((2,)),
+            dma((6,)),
             dma,
             dma,
             dma((depth, 2, 2)),
             dma((depth, 2, 2)),
             dma((depth, 2, 2)),
             dma((depth, 2, 2)),
-            dma((7,)),
-            dma((2, 2, 2)),
+            dma((7, 2)),
+            dma((2, 2, 2, 2)),
             dma((group,)),
             dma((group,)),
             dma((subs,)),
             dma((subs,)),
             dma((subs,)),
             dma((2,)),
+            pltpu.SemaphoreType.REGULAR((depth - 2,)),
+            pltpu.SemaphoreType.REGULAR((depth - 2,)),
         ],
         compiler_params=pltpu.CompilerParams(
-            collective_id=0, has_side_effects=True, vmem_limit_bytes=56 << 20
+            collective_id=0, has_side_effects=True, vmem_limit_bytes=32 << 20
         ),
     )(
-        range_filter,
-        raw_pulses[:, :, 0, :],
-        form,
-        band_offsets[:, None, :],
-        band_weights.transpose(0, 1, 2, 4, 3),
+        *(
+            pltpu.with_memory_space_constraint(array, pltpu.HBM)
+            for array in (
+                range_filter,
+                raw_pulses[:, :, 0, :],
+                channel_mix.transpose(0, 2, 3, 1),
+                steer_angles[None, :],
+                band_offsets,
+                band_weights.transpose(0, 1, 2, 4, 3),
+            )
+        )
     )
     return pl.pallas_call(
         functools.partial(smooth_body, chans),
         out_shape=jax.ShapeDtypeStruct((angles, half), jnp.float32),
         in_specs=[vmem, vmem],
         out_specs=vmem,
+        compiler_params=pltpu.CompilerParams(vmem_limit_bytes=8 << 20),
     )(power, smoothing[None, :])
 
 
@@ -701,7 +833,7 @@
     subs, chans = mesh.shape["sub"], mesh.shape["chan"]
     rows = range_filter.shape[1] // (subs * chans)
     pulses = raw_pulses.shape[1] // subs
-    cut = chans == 2 and subs % 16 == 0 and subs & (subs - 1) == 0
+    cut = chans == 2 and subs // 4 == 4
     cut = cut and range_filter.shape[2] == 4 * chans * LANES and LANES // (subs // 4) >= HALO
     cut = cut and rows % 16 == 0 and pulses % 16 == 0 and steer_angles.shape[0] % LANES == 0
     return cut and band_offsets.shape[0] == 4

time: 50.7 us -> 42.2 us (0.83)
  Pallas kernels: 46 us -> 42.1 us
  local copies, waits for them, and re-layouts: 2.77 us -> 0.01 us
  other arithmetic: 1.2 us -> 0 us
  matrix products: 0.52 us -> 0 us
    pallas_call x1, Pallas kernels: 43.6 us -> 40.7 us  [local_kernel(): pl.pallas_call(functools.partial(window_body, subs), out_shape=jax.ShapeD...]
    unnamed x6 -> x2, local copies, waits for them, and re-layouts: 1.95 us -> 0.01 us
    pallas_call x1, Pallas kernels: 2.32 us -> 1.36 us  [local_kernel(): pl.pallas_call(functools.partial(smooth_body, chans), out_shape=jax.Shape...]
    concatenate x1 -> x0, other arithmetic: 0.73 us -> none  [forming_rows(): return jnp.concatenate([top, low], axis=0)]
    broadcast_in_dim x1 -> x0, local copies, waits for them, and re-layouts: 0.61 us -> none  [local_kernel(): band_offsets[:, None, :]]
    dot_general x2 -> x0, matrix products: 0.52 us -> none  [the longest x1 0.26 us: forming_rows(): jnp.dot(left, jnp.concatenate([beam_i, beam_r], axis=0), precision=HIGH)]
where the time goes in v2:
time: 42.2 us; the launch traced here: 42.1 us
  Pallas kernels  42.1 us (100%)
    pallas_call x1, Pallas kernels, local_kernel(): pl.pallas_call(functools.partial(window_body, subs), out_shape=jax.ShapeD...  40.7 us
    pallas_call x1, Pallas kernels, local_kernel(): pl.pallas_call(functools.partial(smooth_body, chans), out_shape=jax.Shape...  1.36 us

profile of v2, /device:TPU:0, one launch (start us, length us, event | category | flops | bytes accessed | tf_op | source)
XLA Modules:
  0.0 42.1 jit_solution(17186210369728929001)
XLA Ops:
  0.0 0.0 copy-start
  0.0 40.7 %shard_map.73.power_ref = bf16[544,256]{1,0:T(8,128)(2,1)S(1)} custom-call(bf16[2,64,1024]{2,1,0:T(8,128)(2,1)} %filt_hbm.1, bf16[2,32,2048]{2,1,0:T(8,128)(2,1)} %bitcast.6, f32[2,2,2,32]{3,2,1,0:T(2,128)} %bitcast.8, f32[1,256]{1,0:T(1,128)} %bitcast.9, s32[4,512]{1,0:T(4,128)} %offs_hbm.1, f32[4,2,2,8,512]{4,3,2,1,0:T(8,128)} %bitcast.7), custom_call_target="tpu_custom_call" | custom-call | tf_op jit(solution)/shard_map/pallas_call | solution.py:763
  40.7 0.0 copy-done
  40.7 1.4 %shard_map.74 = f32[256,512]{1,0:T(8,128)} custom-call(bf16[544,256]{1,0:T(8,128)(2,1)S(1)} %shard_map.73.power_ref, f32[1,256]{1,0:T(1,128)S(1)} %bitcast.5), custom_call_target="tpu_custom_call" | custom-call | tf_op jit(solution)/shard_map/pallas_call | solution.py:823
Async XLA Ops:
  0.0 40.7 %copy-start = (f32[256]{0:T(256)S(1)}, f32[256]{0:T(256)}, u32[]{:S(2)}) copy-start(f32[256]{0:T(256)} %param.13) | copy-start | bytes 3076

commit v3 on v2

--- a/solution.py
+++ b/solution.py
@@ -240,7 +240,7 @@
     steer_hbm,
     offs_hbm,
     wts_hbm,
-    out_ref,
+    rows_c,
     mix_ref,
     steer_ref,
     offs_ref,
@@ -260,7 +260,6 @@
     img_a,
     img_b,
     pbuf,
-    rows_c,
     loc_sem,
     y_s,
     y_r,
@@ -482,19 +481,19 @@
         value = low_dot(left, right)
         acc[...] = value if fresh else acc[...] + value
 
+    other = pl.multiple_of((1 - c) * half, half)
     load_b.wait()
-    other = pl.multiple_of((1 - c) * half, half)
     go(remote(bsrc.at[:, :, pl.ds(other, half)], ys, y_s, y_r, device(0, 0, 0, 1)))
     kept = keep(0)
     go(block(0, 1, 0))
     load_a.wait()
     pass_echo(0, (0, 0, 0), (1, 0, 0), (1, 0, 0, 0), 0)
-    for part in range(2):
-        pass_echo(1, (0, 0, 0), (0, 0, 1), (0, 0, 0, 1), part)
+    pass_echo(1, (0, 0, 0), (0, 0, 1), (0, 0, 0, 1), 0)
+    pass_echo(1, (0, 0, 0), (0, 0, 1), (0, 0, 0, 1), 1)
     for dk in range(2):
         go(block(1, dk, 0))
-    for part in range(2):
-        pass_echo(2, (0, 0, 0), (0, 1, 0), (0, 0, 1, 0), part)
+    pass_echo(2, (0, 0, 0), (0, 1, 0), (0, 0, 1, 0), 0)
+    pass_echo(2, (0, 0, 0), (0, 1, 0), (0, 0, 1, 0), 1)
     far_pairs = [block(turn, dk, 0) for turn in range(2, depth) for dk in range(2)]
     sent.extend(far_pairs)
 
@@ -527,13 +526,15 @@
             copy.start()
 
     pass_echo(0, (0, 0, 0), (1, 0, 0), (1, 0, 0, 0), 1)
-
     remote(ys, ys, y_s, y_r, device(0, 0, 0, 1)).wait_recv()
     kept = keep(1)
     go(block(0, 1, 1))
-    for dk in range(2):
-        for turn in range(1, depth):
-            go(block(turn, dk, 1))
+    go(block(1, 0, 1))
+    go(block(1, 1, 1))
+    go(block(2, 0, 1))
+    go(block(2, 1, 1))
+    go(block(3, 0, 1))
+    go(block(3, 1, 1))
     kept.wait()
     go(across(0, 0, 1))
     for table in tables:
@@ -546,23 +547,45 @@
         pass_echo(3, (1, 0, 0), (1, 0, 1), (0, 0, 0, 1), part)
         pass_echo(4, (1, 0, 0), (1, 1, 0), (0, 0, 1, 0), part)
 
+    def relay_side():
+        for part in range(2):
+            echo_in(0, 0, 1, part)
+            pass_echo(5, (0, 0, 1), (0, 1, 1), (0, 0, 1, 0), part)
+
     relay(0)
     arrived(0, 1, 1)
     go(across(0, 1, 1))
-    for dc in range(2):
-        for dk in range(2):
-            for turn in range(1, depth):
-                arrived(turn, dk, dc)
-                go(across(turn, dk, dc))
-            if pending:
-                build(*pending.pop(0))
-            if dc == 0 and dk == 1:
-                fold()
-        if dc == 0:
-            relay(1)
-            for part in range(2):
-                echo_in(0, 0, 1, part)
-                pass_echo(5, (0, 0, 1), (0, 1, 1), (0, 0, 1, 0), part)
+    arrived(1, 0, 0)
+    go(across(1, 0, 0))
+    arrived(2, 0, 0)
+    go(across(2, 0, 0))
+    arrived(3, 0, 0)
+    go(across(3, 0, 0))
+    build(*pending.pop(0))
+    arrived(1, 1, 0)
+    go(across(1, 1, 0))
+    arrived(2, 1, 0)
+    go(across(2, 1, 0))
+    arrived(3, 1, 0)
+    go(across(3, 1, 0))
+    build(*pending.pop(0))
+    fold()
+    relay(1)
+    arrived(1, 0, 1)
+    go(across(1, 0, 1))
+    arrived(1, 1, 1)
+    go(across(1, 1, 1))
+    arrived(2, 0, 1)
+    go(across(2, 0, 1))
+    build(*pending.pop(0))
+    relay_side()
+    arrived(2, 1, 1)
+    go(across(2, 1, 1))
+    arrived(3, 0, 1)
+    go(across(3, 0, 1))
+    arrived(3, 1, 1)
+    go(across(3, 1, 1))
+    build(*pending.pop(0))
     for part in range(2):
         echo_in(1, 0, 1, part)
         pass_echo(6, (1, 0, 1), (1, 1, 1), (0, 0, 1, 0), part)
@@ -595,6 +618,8 @@
             to = flip(zp, dzp) * 2 + flip(x, dx)
             go(remote(sbuf.at[to], img0.at[mine], sb_s.at[slot], sb_r.at[slot], device(2 * dzp, dx, 0, 0)))
     img0[mine] = sbuf[mine]
+    while len(sent) > group - 1:
+        sent.pop(0).wait_send()
     for dzp, dx in spread:
         slot = dzp * 2 + dx
         if slot:
@@ -659,28 +684,6 @@
                         )
                     )
 
-    def halo(slot, up):
-        dzp, rel = slot // 8, slot % 8
-        dx, dzz, dk = rel // 4, (rel // 2) % 2, rel % 2
-        src = pbuf.at[flip(zp, dzp), flip(x, dx), flip(par, dzz), flip(k, dk)]
-        src = src.at[pl.ds(own - HALO if up else 0, HALO), :]
-        dst = rows_c.at[pl.ds(0 if up else HALO + half, HALO), :]
-        return remote(src, dst, h_s.at[slot], h_r.at[0 if up else 1], device(2 * dzp + dzz, dx, dk, 1))
-
-    order = list(range(subs - 1, -1, -1))
-    sends_up = jnp.logical_and(c == 0, base == HALO + half - own)
-    sends_down = jnp.logical_and(c == 1, base == HALO)
-
-    @pl.when(sends_up)
-    def _():
-        for slot in order:
-            halo(slot, True).start()
-
-    @pl.when(sends_down)
-    def _():
-        for slot in order:
-            halo(slot, False).start()
-
     rows_c[pl.ds(block_at, own), :] = pbuf[zp, x, par, k]
 
     @pl.when(c == 0)
@@ -691,56 +694,69 @@
     def _():
         rows_c[pl.ds(HALO + half, HALO), :] = jnp.zeros((HALO, angles), LOW)
 
-    for slot in order:
-        if slot:
-            dzp, rel = slot // 8, slot % 8
-            dx, dzz, dk = rel // 4, (rel // 2) % 2, rel % 2
-            origin = (flip(par, dzz) * 2 + flip(k, dk)) * group + flip(zp, dzp) * 2 + flip(x, dx)
-            at = pl.multiple_of(HALO + origin * own, HALO)
-            dst = rows_c.at[pl.ds(at, own), :]
-            remote(
-                dst, dst, sc_s.at[slot], sc_r.at[slot], device(2 * dzp + dzz, dx, dk, 0)
-            ).wait_recv()
-
-    @pl.when(c == 1)
+    def landed(slot):
+        dzp, rel = slot // 8, slot % 8
+        at_zp, at_x = across_bit(zp, dzp), across_bit(x, rel // 4)
+        at_par, at_k = across_bit(par, (rel // 2) % 2), across_bit(k, rel % 2)
+        at = HALO + ((at_par * 2 + at_k) * group + at_zp * 2 + at_x) * own
+        dst = rows_c.at[pl.ds(pl.multiple_of(at, HALO), own), :]
+        remote(dst, dst, sc_s.at[slot], sc_r.at[slot], device(0, 0, 0, 1)).wait_recv()
+
+    def across_bit(bit, change):
+        return bit + change - 2 * bit * change
+
+    here = ((zp * 2 + x) * 2 + par) * 2 + k
+    edge = here * c + (subs - 1 - here) * (1 - c)
+
+    @pl.when(edge != 0)
     def _():
-        halo(0, True).wait_recv()
-
-    @pl.when(c == 0)
-    def _():
-        halo(0, False).wait_recv()
-
-    out_ref[...] = rows_c[...]
-
+        landed(edge)
+
+    border = remote(
+        rows_c.at[pl.ds(pl.multiple_of(half * (1 - c) + HALO * c, HALO), HALO), :],
+        rows_c.at[pl.ds(pl.multiple_of((HALO + half) * c, HALO), HALO), :],
+        h_s,
+        h_r,
+        device(0, 0, 0, 1),
+    )
+    border.start()
+    for slot in range(subs - 1, 0, -1):
+
+        @pl.when(edge != slot)
+        def _():
+            landed(slot)
+
+    far_border = rows_c.at[pl.ds(pl.multiple_of((HALO + half) * (1 - c), HALO), HALO), :]
+    remote(far_border, far_border, h_s, h_r, device(0, 0, 0, 1)).wait_recv()
+    border.wait_send()
     for copy in sent:
         copy.wait_send()
 
-    @pl.when(sends_up)
-    def _():
-        for slot in order:
-            halo(slot, True).wait_send()
-
-    @pl.when(sends_down)
-    def _():
-        for slot in order:
-            halo(slot, False).wait_send()
-
-
-def smooth_body(chans, power_ref, rate_ref, out_ref):
+
+def smooth_body(chans, power_ref, rate_ref, out_hbm, turned, sem):
     at = lax.axis_index("chan")
-    power = power_ref[...].astype(jnp.float32)
-    rate = rate_ref[...]
-    height = power.shape[0] - 2 * HALO
-    row = lax.broadcasted_iota(jnp.int32, power.shape, 0)
+    height = turned.shape[1]
+    shape = (height + 2 * HALO, LANES)
+    row = lax.broadcasted_iota(jnp.int32, shape, 0)
     inside = jnp.logical_and(
         jnp.logical_or(row >= HALO, at > 0), jnp.logical_or(row < HALO + height, at < chans - 1)
     )
-    for sweep in range(PASSES):
-        before = jnp.concatenate([power[:1], power[:-1]], axis=0)
-        after = jnp.concatenate([power[1:], power[-1:]], axis=0)
-        power = power + rate * (before - 2.0 * power + after)
-        power = jnp.where(inside, power, 0.0)
-    out_ref[...] = power[HALO : HALO + height].T
+    copies = []
+    for part in range(turned.shape[0] // LANES):
+        cols = slice(part * LANES, (part + 1) * LANES)
+        power = power_ref[:, cols].astype(jnp.float32)
+        rate = rate_ref[:, cols]
+        for sweep in range(PASSES):
+            before = pltpu.roll(power, 1, 0)
+            after = pltpu.roll(power, shape[0] - 1, 0)
+            power = power + rate * (before - 2.0 * power + after)
+            power = jnp.where(inside, power, 0.0)
+        turned[cols, :] = power[HALO : HALO + height].T
+        copy = pltpu.make_async_copy(turned.at[cols, :], out_hbm.at[cols, :], sem.at[part])
+        copy.start()
+        copies.append(copy)
+    for copy in copies:
+        copy.wait()
 
 
 def local_kernel(
@@ -785,7 +801,6 @@
             pltpu.VMEM(place + (own, 2 * angles), LOW),
             pltpu.VMEM(place + (own, 2 * angles), LOW),
             pltpu.VMEM(place + (own, angles), LOW),
-            pltpu.VMEM((half + 2 * HALO, angles), LOW),
             dma((6,)),
             dma,
             dma,
@@ -799,8 +814,8 @@
             dma((group,)),
             dma((subs,)),
             dma((subs,)),
-            dma((subs,)),
-            dma((2,)),
+            dma,
+            dma,
             pltpu.SemaphoreType.REGULAR((depth - 2,)),
             pltpu.SemaphoreType.REGULAR((depth - 2,)),
         ],
@@ -824,7 +839,8 @@
         functools.partial(smooth_body, chans),
         out_shape=jax.ShapeDtypeStruct((angles, half), jnp.float32),
         in_specs=[vmem, vmem],
-        out_specs=vmem,
+        out_specs=anywhere,
+        scratch_shapes=[pltpu.VMEM((angles, half), jnp.float32), dma((angles // LANES,))],
         compiler_params=pltpu.CompilerParams(vmem_limit_bytes=8 << 20),
     )(power, smoothing[None, :])
 

time: 42.2 us -> 41.1 us (0.974)
  Pallas kernels: 42.1 us -> 41 us
    pallas_call x1, Pallas kernels: 40.7 us -> 39.7 us  [local_kernel(): pl.pallas_call(functools.partial(window_body, subs), out_shape=jax.ShapeD...]
where the time goes in v3:
time: 41.1 us; the launch traced here: 41 us
  Pallas kernels  41 us (100%)
    pallas_call x1, Pallas kernels, local_kernel(): pl.pallas_call(functools.partial(window_body, subs), out_shape=jax.ShapeD...  39.7 us
    pallas_call x1, Pallas kernels, local_kernel(): pl.pallas_call(functools.partial(smooth_body, chans), out_shape=jax.Shape...  1.29 us

profile of v3, /device:TPU:0, one launch (start us, length us, event | category | flops | bytes accessed | tf_op | source)
XLA Modules:
  0.0 41.0 jit_solution(2132688699136906609)
XLA Ops:
  0.0 0.0 copy-start
  0.0 39.7 %shard_map.73.power_ref = bf16[544,256]{1,0:T(8,128)(2,1)S(1)} custom-call(bf16[2,64,1024]{2,1,0:T(8,128)(2,1)} %filt_hbm.1, bf16[2,32,2048]{2,1,0:T(8,128)(2,1)} %bitcast.6, f32[2,2,2,32]{3,2,1,0:T(2,128)} %bitcast.8, f32[1,256]{1,0:T(1,128)} %bitcast.9, s32[4,512]{1,0:T(4,128)} %offs_hbm.1, f32[4,2,2,8,512]{4,3,2,1,0:T(8,128)} %bitcast.7), custom_call_target="tpu_custom_call" | custom-call | tf_op jit(solution)/shard_map/pallas_call | solution.py:779
  39.7 0.0 copy-done
  39.7 1.3 %shard_map.74 = f32[256,512]{1,0:T(8,128)} custom-call(bf16[544,256]{1,0:T(8,128)(2,1)S(1)} %shard_map.73.power_ref, f32[1,256]{1,0:T(1,128)S(1)} %bitcast.5), custom_call_target="tpu_custom_call" | custom-call | tf_op jit(solution)/shard_map/pallas_call | solution.py:838
Async XLA Ops:
  0.0 39.7 %copy-start = (f32[256]{0:T(256)S(1)}, f32[256]{0:T(256)}, u32[]{:S(2)}) copy-start(f32[256]{0:T(256)} %param.13) | copy-start | bytes 3076

commit v4 on v3

--- a/solution.py
+++ b/solution.py
@@ -669,7 +669,7 @@
             pbuf[pair_at * 2 + side] = power[pair_at]
         for high in range(place[0] // 2):
             dzp = high * 2 + turn
-            for rel in range(8):
+            for rel in (0, 4, 1, 5, 2, 6, 3, 7):
                 dx, dzz, dk = rel // 4, (rel // 2) % 2, rel % 2
                 slot = dzp * 8 + rel
                 src = pbuf.at[flip(zp, dzp), flip(x, dx), flip(par, dzz), flip(k, dk)]

time: 41.1 us -> 40.1 us (0.976)
  Pallas kernels: 41 us -> 40 us
    pallas_call x1, Pallas kernels: 39.7 us -> 38.7 us  [local_kernel(): pl.pallas_call(functools.partial(window_body, subs), out_shape=jax.ShapeD...]
where the time goes in v4:
time: 40.1 us; the launch traced here: 40 us
  Pallas kernels  40 us (100%)
    pallas_call x1, Pallas kernels, local_kernel(): pl.pallas_call(functools.partial(window_body, subs), out_shape=jax.ShapeD...  38.7 us
    pallas_call x1, Pallas kernels, local_kernel(): pl.pallas_call(functools.partial(smooth_body, chans), out_shape=jax.Shape...  1.29 us

profile of v4, /device:TPU:0, one launch (start us, length us, event | category | flops | bytes accessed | tf_op | source)
XLA Modules:
  0.0 40.0 jit_solution(18026455181009074450)
XLA Ops:
  0.0 0.0 copy-start
  0.0 38.7 %shard_map.73.power_ref = bf16[544,256]{1,0:T(8,128)(2,1)S(1)} custom-call(bf16[2,64,1024]{2,1,0:T(8,128)(2,1)} %filt_hbm.1, bf16[2,32,2048]{2,1,0:T(8,128)(2,1)} %bitcast.6, f32[2,2,2,32]{3,2,1,0:T(2,128)} %bitcast.8, f32[1,256]{1,0:T(1,128)} %bitcast.9, s32[4,512]{1,0:T(4,128)} %offs_hbm.1, f32[4,2,2,8,512]{4,3,2,1,0:T(8,128)} %bitcast.7), custom_call_target="tpu_custom_call" | custom-call | tf_op jit(solution)/shard_map/pallas_call | solution.py:779
  38.7 0.0 copy-done
  38.7 1.3 %shard_map.74 = f32[256,512]{1,0:T(8,128)} custom-call(bf16[544,256]{1,0:T(8,128)(2,1)S(1)} %shard_map.73.power_ref, f32[1,256]{1,0:T(1,128)S(1)} %bitcast.5), custom_call_target="tpu_custom_call" | custom-call | tf_op jit(solution)/shard_map/pallas_call | solution.py:838
Async XLA Ops:
  0.0 38.7 %copy-start = (f32[256]{0:T(256)S(1)}, f32[256]{0:T(256)}, u32[]{:S(2)}) copy-start(f32[256]{0:T(256)} %param.13) | copy-start | bytes 3076
